TPU v7x, 16 devices: a whole 2x2x2 slice. The times are simulated.
16 devices in a mesh: rep: 1, dp: 16 (over x, y, z, core).
Axes of the slice: x: 2, y: 2, z: 2, core: 2. Of those that a mesh axis runs over, the one named last changes fastest.
Arguments:
- x: bfloat16 [16, 2048, 768], P(('rep', 'dp'))
- dy: bfloat16 [16, 2048, 768], P(('rep', 'dp'))
- w_gate: bfloat16 [2, 768, 3072], replicated
- w_up: bfloat16 [2, 768, 3072], replicated
- w_down: bfloat16 [2, 3072, 768], replicated
- m_w_gate: float32 [2, 768, 3072], P(None, 'dp')
- m_w_up: float32 [2, 768, 3072], P(None, 'dp')
- m_w_down: float32 [2, 3072, 768], P(None, 'dp')
- v_w_gate: float32 [2, 768, 3072], P(None, 'dp')
- v_w_up: float32 [2, 768, 3072], P(None, 'dp')
- v_w_down: float32 [2, 3072, 768], P(None, 'dp')
Outputs:
- output 1: bfloat16 [2, 768, 3072], P('rep')
- output 2: bfloat16 [2, 768, 3072], P('rep')
- output 3: bfloat16 [2, 3072, 768], P('rep')
- output 4: float32 [2, 768, 3072], P('rep', 'dp')
- output 5: float32 [2, 768, 3072], P('rep', 'dp')
- output 6: float32 [2, 3072, 768], P('rep', 'dp')
- output 7: float32 [2, 768, 3072], P('rep', 'dp')
- output 8: float32 [2, 768, 3072], P('rep', 'dp')
- output 9: float32 [2, 3072, 768], P('rep', 'dp')
All inputs are finite; a program needn't handle non-finite values.
Results may differ from a plain program's by a relative error of at most 0.022.
Values are sent between devices in bfloat16 or wider.
A program may use at most 2 GiB of HBM per device.

v0:
```python
import jax
import jax.numpy as jnp
from jax import lax

NAMES = ("w_gate", "w_up", "w_down")


def matmul(a, w):
    return jnp.dot(a, w, preferred_element_type=jnp.float32).astype(jnp.bfloat16)


def normed(h):
    wide = h.astype(jnp.float32)
    scale = lax.rsqrt(jnp.mean(wide**2, -1, keepdims=True) + 1e-6)
    return (wide * scale).astype(jnp.bfloat16)


def layer(h, w):
    a = normed(h)
    gate = jnp.dot(a, w["w_gate"], preferred_element_type=jnp.float32)
    up = jnp.dot(a, w["w_up"], preferred_element_type=jnp.float32)
    return h + matmul((jax.nn.silu(gate) * up).astype(jnp.bfloat16), w["w_down"])


def adamw(w, m, v, g):
    m = 0.9 * m + 0.1 * g
    v = 0.95 * v + 0.05 * g * g
    step = m * lax.rsqrt(v + 1e-8) + 0.1 * w
    return (w - 0.02 * step).astype(jnp.bfloat16), m, v


def stack(weights, h):
    for number in range(weights["w_gate"].shape[0]):
        h = layer(h, {name: w[number] for name, w in weights.items()})
    return h


def solution(mesh):
    groups = mesh.shape["rep"]

    def step(x, dy, *arrays):
        weights, m, v = (arrays[i : i + 3] for i in (0, 3, 6))
        x, dy = (t.reshape(groups, -1, *t.shape[1:]) for t in (x, dy))

        def of_a_group(x, dy):
            _, back = jax.vjp(lambda w: stack(w, x), dict(zip(NAMES, weights, strict=True)))
            by_weights = back(dy)[0]
            gradients = [by_weights[name].astype(jnp.float32) for name in NAMES]
            new = [adamw(w.astype(jnp.float32), m, v, g) for w, m, v, g in zip(weights, m, v, gradients, strict=True)]
            return tuple(one[which] for which in range(3) for one in new)

        return tuple(t.reshape(-1, *t.shape[2:]) for t in jax.vmap(of_a_group)(x, dy))

    return step
```

profile of v0, /device:TPU:0, one launch (start us, length us, event | category | flops | bytes accessed | tf_op | source)
XLA Modules:
  0.0 1281.4 jit_solution(14921839626720283387)
XLA Ops:
  14.1 14.0 %fusion.177 = f32[2048,3072]{1,0:T(8,128)} fusion(bf16[2,768,3072]{2,1,0:T(8,128)(2,1)S(1)} %copy-done.21, bf16[1,2048,768]{1,2,0:T(8,128)(2,1)S(1)} %fusion.161), kind=kOutput, calls=%fused_computation.224 | convolution fusion | flops 9663676416 | bytes 33030144 | tf_op jit(solution)/vmap(jvp())/dot_general | solution.py:20
  28.1 26.2 %fusion.154 = (bf16[1,2048,3072]{2,1,0:T(8,128)(2,1)}, f32[2048,3072]{1,0:T(8,128)}) fusion(f32[2048,3072]{1,0:T(8,128)} %fusion.177, bf16[2,768,3072]{2,1,0:T(8,128)(2,1)} %param.17, bf16[1,2048,768]{1,2,0:T(8,128)(2,1)S(1)} %fusion.161), kind=kOutput, calls=%fused_computation.189 | convolution fusion | flops 9701425152 | bytes 70778880 | tf_op jit(solution)/vmap(jvp())/dot_general | solution.py:21
  54.3 15.0 %fusion.164 = (f32[2048]{0:T(1024)S(1)}, bf16[1,2048,768]{1,2,0:T(8,128)(2,1)S(1)}) fusion(bf16[1,2048,768]{1,2,0:T(8,128)(2,1)S(1)} %copy.1, bf16[2,3072,768]{2,1,0:T(8,128)(2,1)} %param.15, bf16[1,2048,3072]{2,1,0:T(8,128)(2,1)} %get-tuple-element.263), kind=kOutput, calls=%fused_computation.211 | convolution fusion | flops 9671538688 | bytes 23601152 | tf_op jit(solution)/vmap(jvp())/dot_general | solution.py:9
  71.0 17.0 %fusion.170 = f32[2048,3072]{1,0:T(8,128)} fusion(bf16[2,768,3072]{2,1,0:T(8,128)(2,1)} %param.17, bf16[1,2048,768]{1,2,0:T(8,128)(2,1)S(1)} %fusion.165), kind=kOutput, calls=%fused_computation.217 | convolution fusion | flops 9663676416 | bytes 33030144 | tf_op jit(solution)/vmap(jvp())/dot_general | solution.py:21
  88.0 14.7 %convolution_convert_fusion.1 = bf16[2048,3072]{1,0:T(8,128)(2,1)} fusion(bf16[2,3072,768]{2,1,0:T(8,128)(2,1)} %param.15, bf16[1,2048,768]{2,1,0:T(8,128)(2,1)S(1)} %copy-done.5), kind=kOutput, calls=%fused_computation.199 | convolution fusion | flops 9669967872 | bytes 20447232 | tf_op jit(solution)/vmap(transpose(jvp()))/dot_general | solution.py:9
  102.7 36.7 %fusion.143 = (bf16[1,2048,3072]{2,1,0:T(8,128)(2,1)}, bf16[1,2048,3072]{2,1,0:T(8,128)(2,1)}, f32[2048,3072]{1,0:T(8,128)}) fusion(f32[2048,3072]{1,0:T(8,128)} %fusion.170, bf16[2048,3072]{1,0:T(8,128)(2,1)} %convolution_convert_fusion.1, bf16[2,768,3072]{2,1,0:T(8,128)(2,1)} %param.12, bf16[1,2048,768]{1,2,0:T(8,128)(2,1)S(1)} %fusion.165), kind=kOutput, calls=%fused_computation.173 | convolution fusion | flops 9758048256 | bytes 95944704 | tf_op jit(solution)/vmap(jvp())/dot_general | solution.py:20
  139.4 21.7 %fusion.153 = bf16[1,2048,3072]{2,1,0:T(8,128)(2,1)} fusion(f32[2048,3072]{1,0:T(8,128)} %fusion.170, f32[2048,3072]{1,0:T(8,128)} %get-tuple-element.267), kind=kLoop, calls=%fused_computation.187 | loop fusion | flops 37748736 | bytes 62914560 | tf_op jit(solution)/vmap(jvp())/convert_element_type | solution.py:22
  161.1 16.8 %copy.3 = bf16[1,2048,3072]{1,2,0:T(8,128)(2,1)} copy(bf16[1,2048,3072]{2,1,0:T(8,128)(2,1)} %fusion.153) | data formatting | bytes 25165824
  177.9 141.8 %while.16 = (bf16[1,2048,3072]{1,2,0:T(8,128)(2,1)}, bf16[1,2048,768]{2,1,0:T(8,128)(2,1)S(1)}, f32[192,768]{1,0:T(8,128)}, f32[192,768]{1,0:T(8,128)}, u32[]{:T...) while((bf16[1,2048,3072]{1,2,0:T(8,128)(2,1)}, ...), condition=%wide.windowed_dot_general_cond_rs.4.clone, body=%wide.windowed_dot_general_body_rs.4.clone.sunk | while | flops 2423095296 | bytes 52691536 | solution.py:9
  329.9 16.7 %copy.5 = bf16[1,2048,3072]{1,2,0:T(8,128)(2,1)} copy(bf16[1,2048,3072]{2,1,0:T(8,128)(2,1)} %get-tuple-element.263) | data formatting | bytes 25165824
  346.5 14.9 %fusion.194 = bf16[2048,768]{0,1:T(8,128)(2,1)S(1)} fusion(bf16[2,768,3072]{2,1,0:T(8,128)(2,1)} %param.17, bf16[1,2048,3072]{2,1,0:T(8,128)(2,1)} %get-tuple-element.612), kind=kOutput, calls=%fused_computation.237 | convolution fusion | flops 9663676416 | bytes 20447232 | tf_op jit(solution)/vmap(transpose(jvp()))/dot_general | solution.py:21
  361.5 14.9 %fusion.166 = (f32[2048]{0:T(1024)S(1)}, bf16[2048,768]{0,1:T(8,128)(2,1)S(1)}) fusion(bf16[1,2048,768]{1,2,0:T(8,128)(2,1)S(1)} %copy-done.9, bf16[2048,768]{0,1:T(8,128)(2,1)S(1)} %fusion.194, bf16[2,768,3072]{2,1,0:T(8,128)(2,1)} %param.12, bf16[1,2048,3072]{2,1,0:T(8,128)(2,1)} %get-tuple-element.540), kind=kOutput, calls=%fused_computation.213 | convolution fusion | flops 9671538688 | bytes 26746880 | tf_op jit(solution)/vmap(transpose(jvp()))/dot_general | solution.py:20
  382.0 140.0 %while.17 = (bf16[1,2048,768]{2,1,0:T(8,128)(2,1)}, bf16[1,2048,3072]{1,2,0:T(8,128)(2,1)}, f32[768,192]{0,1:T(8,128)}, f32[768,192]{0,1:T(8,128)}, u32[]{:T(128...) while((bf16[1,2048,768]{2,1,0:T(8,128)(2,1)}, ...), condition=%wide.windowed_dot_general_cond_rs.5.clone, body=%wide.windowed_dot_general_body_rs.5.clone.sunk | while | flops 2423095296 | bytes 52691536 | solution.py:9
  529.5 136.4 %while.14 = (bf16[1,2048,3072]{2,1,0:T(8,128)(2,1)}, bf16[1,2048,768]{1,2,0:T(8,128)(2,1)S(1)}, f32[3072,48]{0,1:T(8,128)}, f32[3072,48]{0,1:T(8,128)}, u32[]{:T...) while((bf16[1,2048,3072]{2,1,0:T(8,128)(2,1)}, ...), condition=%wide.windowed_dot_general_cond_rs.2.clone, body=%wide.windowed_dot_general_body_rs.2.clone.sunk | while | flops 2418376704 | bytes 52691536 | solution.py:21
  543.5 9.3 collective-permute-start.10
  672.2 35.5 %convert_multiply_fusion = (bf16[1,2048,3072]{2,1,0:T(8,128)(2,1)}, bf16[1,2048,3072]{2,1,0:T(8,128)(2,1)}) fusion(f32[2048,3072]{1,0:T(8,128)} %fusion.177, f32[2048,3072]{1,0:T(8,128)} %get-tuple-element.264, bf16[2,3072,768]{2,1,0:T(8,128)(2,1)} %param.15, bf16[1,2048,768]{1,2,0:T(8,128)(2,1)} %copy-done.7), kind=kOutput, calls=%fused_computation.168 | convolution fusion | flops 9764339712 | bytes 83361792 | tf_op jit(solution)/vmap(transpose(jvp()))/dot_general | solution.py:9
  707.7 128.4 %while.15 = (bf16[1,2048,3072]{2,1,0:T(8,128)(2,1)}, bf16[1,2048,768]{1,2,0:T(8,128)(2,1)S(1)}, f32[3072,48]{0,1:T(8,128)}, f32[3072,48]{0,1:T(8,128)}, u32[]{:T...) while((bf16[1,2048,3072]{2,1,0:T(8,128)(2,1)}, ...), condition=%wide.windowed_dot_general_cond_rs.3.clone, body=%wide.windowed_dot_general_body_rs.3.clone.sunk | while | flops 2418376704 | bytes 52691536 | solution.py:21
  848.6 157.0 %while.12 = (bf16[1,2048,3072]{2,1,0:T(8,128)(2,1)}, bf16[1,2048,768]{1,2,0:T(8,128)(2,1)}, f32[3072,48]{0,1:T(8,128)}, f32[3072,48]{0,1:T(8,128)}, u32[]{:T(128...) while((bf16[1,2048,3072]{2,1,0:T(8,128)(2,1)}, ...), condition=%wide.windowed_dot_general_cond_rs.clone, body=%wide.windowed_dot_general_body_rs.clone.sunk | while | flops 2418376704 | bytes 65274476 | solution.py:20
  879.1 9.1 collective-permute-done.3
  906.7 13.1 %collective-permute-done.1 = f32[3072,48]{0,1:T(8,128)} collective-permute-done((f32[3072,48]{0,1:T(8,128)}, f32[3072,48]{0,1:T(8,128)}, u32[]{:S(2)}, u32[]{:S(2)}) %collective-permute-start.1) | collective-permute-done | bytes 589856 | tf_op jit(solution)/vmap(transpose(jvp()))/dot_general | solution.py:20
  1019.2 156.5 %while.13 = (bf16[1,2048,3072]{2,1,0:T(8,128)(2,1)}, bf16[1,2048,768]{1,2,0:T(8,128)(2,1)S(1)}, f32[3072,48]{0,1:T(8,128)}, f32[3072,48]{0,1:T(8,128)}, u32[]{:T...) while((bf16[1,2048,3072]{2,1,0:T(8,128)(2,1)}, ...), condition=%wide.windowed_dot_general_cond_rs.1.clone, body=%wide.windowed_dot_general_body_rs.1.clone.sunk | while | flops 2418376704 | bytes 52691536 | solution.py:20
  1077.1 13.3 %collective-permute-done.5 = f32[3072,48]{0,1:T(8,128)} collective-permute-done((f32[3072,48]{0,1:T(8,128)}, f32[3072,48]{0,1:T(8,128)}, u32[]{:S(2)}, u32[]{:S(2)}) %collective-permute-start.5) | collective-permute-done | bytes 589856 | tf_op jit(solution)/vmap(transpose(jvp()))/dot_general | solution.py:20
  1191.5 58.4 %all-gather.10.cloned.1.call-done = bf16[1,2,768,3072]{3,2,1,0:T(8,128)(2,1)} async-done(((bf16[1,2,48,3072]{3,2,1,0:T(8,128)(2,1)}), bf16[1,2,768,3072]{3,2,1,0:T(8,128)(2,1)}) %all-gather.10.cloned.1.call-update) | async-done | bytes 9437200 | tf_op jit(solution)/reshape | solution.py:52
  1249.9 8.3 copy.63
  (436 shorter events, 910.3 us)
Async XLA Ops:
  7.2 1184.3 %all-gather.14.cloned.1.call-start = ((), (), s32[]{:S(2)}) async-start(), calls=%async_computation.2 | async-start | bytes 10027008 | tf_op jit(solution)/reshape | solution.py:52
  319.7 522.7 %collective-permute-start.28 = (f32[192,768]{1,0:T(8,128)}, f32[192,768]{1,0:T(8,128)}, u32[]{:S(2)}, u32[]{:S(2)}) collective-permute-start(f32[192,768]{1,0:T(8,128)} %get-tuple-element.45), channel_id=32, source_target_pairs={{0,1},{1,2},{2,3},{3,4},{4,5},{5,6},{6,7},{7,8},{8,9},{9,10},{10,1... | collective-permute-start | bytes 1769480 | tf_op jit(solution)/vmap(transpose(jvp()))/dot_general | solution.py:9
  522.0 321.9 %collective-permute-start.29 = (f32[768,192]{0,1:T(8,128)}, f32[768,192]{0,1:T(8,128)}, u32[]{:S(2)}, u32[]{:S(2)}) collective-permute-start(f32[768,192]{0,1:T(8,128)} %get-tuple-element.47), channel_id=38, source_target_pairs={{0,1},{1,2},{2,3},{3,4},{4,5},{5,6},{6,7},{7,8},{8,9},{9,10},{10,1... | collective-permute-start | bytes 1769480 | tf_op jit(solution)/vmap(transpose(jvp()))/dot_general | solution.py:9
  543.5 16.0 %collective-permute-start.10 = (f32[3072,48]{0,1:T(8,128)S(1)}, f32[3072,48]{0,1:T(8,128)S(1)}, u32[]{:S(2)}, u32[]{:S(2)}) collective-permute-start(f32[3072,48]{0,1:T(8,128)S(1)} %get-tuple-element.473), channel_id=18, source_target_pairs={{0,1},{1,2},{2,3},{3,4},{4,5},{5,6},{6,7},{7,8},{8,9},{9,10},{10,1... | collective-permute-start | bytes 1769480 | tf_op jit(solution)/vmap(transpose(jvp()))/dot_general | solution.py:21
  563.3 16.7 %collective-permute-start.8 = (f32[3072,48]{0,1:T(8,128)}, f32[3072,48]{0,1:T(8,128)}, u32[]{:S(2)}, u32[]{:S(2)}) collective-permute-start(f32[3072,48]{0,1:T(8,128)} %broadcast_select_fusion.28), channel_id=16, source_target_pairs={{0,1},{1,2},{2,3},{3,4},{4,5},{5,6},{6,7},{7,8},{8,9},{9,10},{10,1... | collective-permute-start | bytes 1769480 | tf_op jit(solution)/vmap(transpose(jvp()))/dot_general | solution.py:21
  598.3 14.9 %collective-permute-start.8 = (f32[3072,48]{0,1:T(8,128)}, f32[3072,48]{0,1:T(8,128)}, u32[]{:S(2)}, u32[]{:S(2)}) collective-permute-start(f32[3072,48]{0,1:T(8,128)} %broadcast_select_fusion.28), channel_id=16, source_target_pairs={{0,1},{1,2},{2,3},{3,4},{4,5},{5,6},{6,7},{7,8},{8,9},{9,10},{10,1... | collective-permute-start | bytes 1769480 | tf_op jit(solution)/vmap(transpose(jvp()))/dot_general | solution.py:21
  632.1 16.8 %collective-permute-start.8 = (f32[3072,48]{0,1:T(8,128)}, f32[3072,48]{0,1:T(8,128)}, u32[]{:S(2)}, u32[]{:S(2)}) collective-permute-start(f32[3072,48]{0,1:T(8,128)} %broadcast_select_fusion.28), channel_id=16, source_target_pairs={{0,1},{1,2},{2,3},{3,4},{4,5},{5,6},{6,7},{7,8},{8,9},{9,10},{10,1... | collective-permute-start | bytes 1769480 | tf_op jit(solution)/vmap(transpose(jvp()))/dot_general | solution.py:21
  665.9 347.2 %collective-permute-start.26 = (f32[3072,48]{0,1:T(8,128)}, f32[3072,48]{0,1:T(8,128)}, u32[]{:S(2)}, u32[]{:S(2)}) collective-permute-start(f32[3072,48]{0,1:T(8,128)} %get-tuple-element.41), channel_id=19, source_target_pairs={{0,1},{1,2},{2,3},{3,4},{4,5},{5,6},{6,7},{7,8},{8,9},{9,10},{10,1... | collective-permute-start | bytes 1769480 | tf_op jit(solution)/vmap(transpose(jvp()))/dot_general | solution.py:21
  737.7 15.1 %collective-permute-start.12 = (f32[3072,48]{0,1:T(8,128)}, f32[3072,48]{0,1:T(8,128)}, u32[]{:S(2)}, u32[]{:S(2)}) collective-permute-start(f32[3072,48]{0,1:T(8,128)} %broadcast_select_fusion.30), channel_id=22, source_target_pairs={{0,1},{1,2},{2,3},{3,4},{4,5},{5,6},{6,7},{7,8},{8,9},{9,10},{10,1... | collective-permute-start | bytes 1769480 | tf_op jit(solution)/vmap(transpose(jvp()))/dot_general | solution.py:21
  803.0 16.1 %collective-permute-start.12 = (f32[3072,48]{0,1:T(8,128)}, f32[3072,48]{0,1:T(8,128)}, u32[]{:S(2)}, u32[]{:S(2)}) collective-permute-start(f32[3072,48]{0,1:T(8,128)} %broadcast_select_fusion.30), channel_id=22, source_target_pairs={{0,1},{1,2},{2,3},{3,4},{4,5},{5,6},{6,7},{7,8},{8,9},{9,10},{10,1... | collective-permute-start | bytes 1769480 | tf_op jit(solution)/vmap(transpose(jvp()))/dot_general | solution.py:21
  836.1 178.4 %collective-permute-start.27 = (f32[3072,48]{0,1:T(8,128)}, f32[3072,48]{0,1:T(8,128)}, u32[]{:S(2)}, u32[]{:S(2)}) collective-permute-start(f32[3072,48]{0,1:T(8,128)} %get-tuple-element.43), channel_id=25, source_target_pairs={{0,1},{1,2},{2,3},{3,4},{4,5},{5,6},{6,7},{7,8},{8,9},{9,10},{10,1... | collective-permute-start | bytes 1769480 | tf_op jit(solution)/vmap(transpose(jvp()))/dot_general | solution.py:21
  848.6 342.9 %all-gather.12.cloned.1.call-start = ((), (), s32[]{:S(2)}) async-start(), calls=%async_computation.1 | async-start | bytes 10027008 | tf_op jit(solution)/reshape | solution.py:52
  872.4 15.8 %collective-permute-start.3 = (f32[3072,48]{0,1:T(8,128)S(1)}, f32[3072,48]{0,1:T(8,128)S(1)}, u32[]{:S(2)}, u32[]{:S(2)}) collective-permute-start(f32[3072,48]{0,1:T(8,128)S(1)} %get-tuple-element.456), channel_id=4, source_target_pairs={{0,15},{1,0},{2,1},{3,2},{4,3},{5,4},{6,5},{7,6},{8,7},{9,8},{10,9... | collective-permute-start | bytes 1769480 | tf_op jit(solution)/vmap(transpose(jvp()))/dot_general | solution.py:20
  891.3 15.4 %collective-permute-start = (f32[3072,48]{0,1:T(8,128)}, f32[3072,48]{0,1:T(8,128)}, u32[]{:S(2)}, u32[]{:S(2)}) collective-permute-start(f32[3072,48]{0,1:T(8,128)} %broadcast_select_fusion.24), channel_id=3, source_target_pairs={{0,1},{1,2},{2,3},{3,4},{4,5},{5,6},{6,7},{7,8},{8,9},{9,10},{10,1... | collective-permute-start | bytes 1769480 | tf_op jit(solution)/vmap(transpose(jvp()))/dot_general | solution.py:20
  899.8 20.0 %collective-permute-start.1 = (f32[3072,48]{0,1:T(8,128)}, f32[3072,48]{0,1:T(8,128)}, u32[]{:S(2)}, u32[]{:S(2)}) collective-permute-start(f32[3072,48]{0,1:T(8,128)} %broadcast_select_fusion.25), channel_id=2, source_target_pairs={{0,15},{1,0},{2,1},{3,2},{4,3},{5,4},{6,5},{7,6},{8,7},{9,8},{10,9... | collective-permute-start | bytes 1769480 | tf_op jit(solution)/vmap(transpose(jvp()))/dot_general | solution.py:20
  938.0 16.2 %collective-permute-start = (f32[3072,48]{0,1:T(8,128)}, f32[3072,48]{0,1:T(8,128)}, u32[]{:S(2)}, u32[]{:S(2)}) collective-permute-start(f32[3072,48]{0,1:T(8,128)} %broadcast_select_fusion.24), channel_id=3, source_target_pairs={{0,1},{1,2},{2,3},{3,4},{4,5},{5,6},{6,7},{7,8},{8,9},{9,10},{10,1... | collective-permute-start | bytes 1769480 | tf_op jit(solution)/vmap(transpose(jvp()))/dot_general | solution.py:20
  972.8 16.0 %collective-permute-start = (f32[3072,48]{0,1:T(8,128)}, f32[3072,48]{0,1:T(8,128)}, u32[]{:S(2)}, u32[]{:S(2)}) collective-permute-start(f32[3072,48]{0,1:T(8,128)} %broadcast_select_fusion.24), channel_id=3, source_target_pairs={{0,1},{1,2},{2,3},{3,4},{4,5},{5,6},{6,7},{7,8},{8,9},{9,10},{10,1... | collective-permute-start | bytes 1769480 | tf_op jit(solution)/vmap(transpose(jvp()))/dot_general | solution.py:20
  1005.6 178.2 %collective-permute-start.24 = (f32[3072,48]{0,1:T(8,128)}, f32[3072,48]{0,1:T(8,128)}, u32[]{:S(2)}, u32[]{:S(2)}) collective-permute-start(f32[3072,48]{0,1:T(8,128)} %get-tuple-element.37), channel_id=6, source_target_pairs={{0,1},{1,2},{2,3},{3,4},{4,5},{5,6},{6,7},{7,8},{8,9},{9,10},{10,1... | collective-permute-start | bytes 1769480 | tf_op jit(solution)/vmap(transpose(jvp()))/dot_general | solution.py:20
  1019.1 230.7 %all-gather.10.cloned.1.call-start = ((), (), s32[]{:S(2)}) async-start(), calls=%async_computation | async-start | bytes 10027008 | tf_op jit(solution)/reshape | solution.py:52
  1043.1 15.8 %collective-permute-start.7 = (f32[3072,48]{0,1:T(8,128)S(1)}, f32[3072,48]{0,1:T(8,128)S(1)}, u32[]{:S(2)}, u32[]{:S(2)}) collective-permute-start(f32[3072,48]{0,1:T(8,128)S(1)} %get-tuple-element.465), channel_id=10, source_target_pairs={{0,15},{1,0},{2,1},{3,2},{4,3},{5,4},{6,5},{7,6},{8,7},{9,8},{10,9... | collective-permute-start | bytes 1769480 | tf_op jit(solution)/vmap(transpose(jvp()))/dot_general | solution.py:20
  1062.0 15.1 %collective-permute-start.4 = (f32[3072,48]{0,1:T(8,128)}, f32[3072,48]{0,1:T(8,128)}, u32[]{:S(2)}, u32[]{:S(2)}) collective-permute-start(f32[3072,48]{0,1:T(8,128)} %broadcast_select_fusion.26), channel_id=9, source_target_pairs={{0,1},{1,2},{2,3},{3,4},{4,5},{5,6},{6,7},{7,8},{8,9},{9,10},{10,1... | collective-permute-start | bytes 1769480 | tf_op jit(solution)/vmap(transpose(jvp()))/dot_general | solution.py:20
  1070.4 20.0 %collective-permute-start.5 = (f32[3072,48]{0,1:T(8,128)}, f32[3072,48]{0,1:T(8,128)}, u32[]{:S(2)}, u32[]{:S(2)}) collective-permute-start(f32[3072,48]{0,1:T(8,128)} %broadcast_select_fusion.27), channel_id=8, source_target_pairs={{0,15},{1,0},{2,1},{3,2},{4,3},{5,4},{6,5},{7,6},{8,7},{9,8},{10,9... | collective-permute-start | bytes 1769480 | tf_op jit(solution)/vmap(transpose(jvp()))/dot_general | solution.py:20
  1108.7 15.3 %collective-permute-start.4 = (f32[3072,48]{0,1:T(8,128)}, f32[3072,48]{0,1:T(8,128)}, u32[]{:S(2)}, u32[]{:S(2)}) collective-permute-start(f32[3072,48]{0,1:T(8,128)} %broadcast_select_fusion.26), channel_id=9, source_target_pairs={{0,1},{1,2},{2,3},{3,4},{4,5},{5,6},{6,7},{7,8},{8,9},{9,10},{10,1... | collective-permute-start | bytes 1769480 | tf_op jit(solution)/vmap(transpose(jvp()))/dot_general | solution.py:20
  1142.9 15.8 %collective-permute-start.4 = (f32[3072,48]{0,1:T(8,128)}, f32[3072,48]{0,1:T(8,128)}, u32[]{:S(2)}, u32[]{:S(2)}) collective-permute-start(f32[3072,48]{0,1:T(8,128)} %broadcast_select_fusion.26), channel_id=9, source_target_pairs={{0,1},{1,2},{2,3},{3,4},{4,5},{5,6},{6,7},{7,8},{8,9},{9,10},{10,1... | collective-permute-start | bytes 1769480 | tf_op jit(solution)/vmap(transpose(jvp()))/dot_general | solution.py:20
  (106 other events, 1211.6 us)
Sparse Core Ops, SparseCore 0:
  848.7 78.8 all-gather.13
  1019.3 78.9 all-gather.11
  1191.5 58.2 all-gather.9
where the time goes:
time: 1290 us; the launch traced here: 1280 us
  matrix products  456 us (35%)
  starting transfers between devices  338 us (26%)
  other arithmetic  202 us (16%)
  waiting for transfers between devices  199 us (15%)
  local copies, waits for them, and re-layouts  70.4 us (5%)
  between operations  14.5 us (1%)
    dot_general x19, matrix products, layer(): gate = jnp.dot(a, w['w_gate'], preferred_element_type=jnp.float32)  173 us
    dot_general x19, matrix products, layer(): up = jnp.dot(a, w['w_up'], preferred_element_type=jnp.float32)  165 us
    dot_general x19, matrix products, matmul(): jnp.dot(a, w, preferred_element_type=jnp.float32).astype(jnp.bfloat16)  117 us
    dot_general x34, starting transfers between devices, matmul(): jnp.dot(a, w, preferred_element_type=jnp.float32).astype(jnp.bfloat16)  113 us
    dot_general x34, starting transfers between devices, layer(): gate = jnp.dot(a, w['w_gate'], preferred_element_type=jnp.float32)  113 us
    dot_general x34, starting transfers between devices, layer(): up = jnp.dot(a, w['w_up'], preferred_element_type=jnp.float32)  113 us
    dot_general x48, other arithmetic  79.4 us
    unnamed x50, local copies, waits for them, and re-layouts  70.4 us
  transfers between devices with their start and end apart: 105, of which 65 were waited for; matrix products, arithmetic and copies ran while one was open for 40% of the time, Pallas kernels for 0%

commit v1 on v0

v1 whole, which is shorter than its diff:
```python
import jax
import jax.numpy as jnp
from jax import lax
from jax.sharding import PartitionSpec as P


def dot(a, b, dims=((1,), (0,))):
    return lax.dot_general(a, b, (dims, ((), ())), preferred_element_type=jnp.float32)


def scale_of(h):
    wide = h.astype(jnp.float32)
    return lax.rsqrt(jnp.mean(wide * wide, -1, keepdims=True) + 1e-6)


def adamw(w, m, v, g):
    m = 0.9 * m + 0.1 * g
    v = 0.95 * v + 0.05 * g * g
    step = m * lax.rsqrt(v + 1e-8) + 0.1 * w
    return (w - 0.02 * step).astype(jnp.bfloat16), m, v


def hidden(gate, up):
    return (jax.nn.silu(gate) * up).astype(jnp.bfloat16)


def back_of_hidden(gate, up, d_s):
    d_s = d_s.astype(jnp.float32)
    sig = jax.nn.sigmoid(gate)
    d_up = d_s * gate * sig
    d_gate = d_s * up * sig * (1 + gate * (1 - sig))
    return d_gate.astype(jnp.bfloat16), d_up.astype(jnp.bfloat16)


def back_of_norm(h, scale, d_a):
    wide, d_a = h.astype(jnp.float32), d_a.astype(jnp.float32)
    dot_ = jnp.mean(d_a * wide, -1, keepdims=True)
    return (d_a * scale - wide * (scale * scale * scale * dot_)).astype(jnp.bfloat16)


def solution(mesh):
    n = mesh.shape["dp"]

    def step(x, dy, wg, wu, wd, mg, mu, md, vg, vu, vd):
        x, dy = x[0], dy[0]
        bf = jnp.bfloat16
        r0 = scale_of(x)
        a0 = (x.astype(jnp.float32) * r0).astype(bf)
        gate0, up0 = dot(a0, wg[0]), dot(a0, wu[0])
        s0 = hidden(gate0, up0)
        h1 = x + dot(s0, wd[0]).astype(bf)
        r1 = scale_of(h1)
        a1 = (h1.astype(jnp.float32) * r1).astype(bf)
        gate1, up1 = dot(a1, wg[1]), dot(a1, wu[1])
        s1 = hidden(gate1, up1)
        g = {}

        def grad(a, b):
            return dot(a, b, ((0,), (0,))).astype(bf)

        def update(name, layer, term, w, m, v):
            total = lax.psum_scatter(term, "dp", scatter_dimension=0, tiled=True).astype(jnp.float32)
            rows = term.shape[0] // n
            mine = lax.dynamic_slice_in_dim(w[layer], lax.axis_index("dp") * rows, rows)
            nw, nm, nv = adamw(mine.astype(jnp.float32), m[layer], v[layer], total)
            g[name, layer] = (lax.all_gather(nw, "dp", axis=0, tiled=True), nm, nv)

        update("d", 1, grad(s1, dy), wd, md, vd)
        ds1 = dot(dy, wd[1], ((1,), (1,))).astype(bf)
        dg1, du1 = back_of_hidden(gate1, up1, ds1)
        update("g", 1, grad(a1, dg1), wg, mg, vg)
        update("u", 1, grad(a1, du1), wu, mu, vu)
        da1 = dot(dg1, wg[1], ((1,), (1,))).astype(bf) + dot(du1, wu[1], ((1,), (1,))).astype(bf)
        dh1 = dy + back_of_norm(h1, r1, da1)
        update("d", 0, grad(s0, dh1), wd, md, vd)
        ds0 = dot(dh1, wd[0], ((1,), (1,))).astype(bf)
        dg0, du0 = back_of_hidden(gate0, up0, ds0)
        update("g", 0, grad(a0, dg0), wg, mg, vg)
        update("u", 0, grad(a0, du0), wu, mu, vu)
        return tuple(jnp.stack([g[name, 0][k], g[name, 1][k]]) for k in range(3) for name in "gud")

    whole, rows = P(None, None, None), P(None, "dp", None)
    return jax.shard_map(
        step,
        mesh=mesh,
        in_specs=(P(("rep", "dp")), P(("rep", "dp")), *[whole] * 3, *[rows] * 6),
        out_specs=(*[P("rep", None, None)] * 3, *[P("rep", "dp", None)] * 6),
        check_vma=False,
    )
```

time: 1290 us -> 807 us (0.63)
  starting transfers between devices: 338 us -> 0.78 us
  waiting for transfers between devices: 199 us -> 419 us
  matrix products: 456 us -> 289 us
  other arithmetic: 202 us -> 44.7 us
  local copies, waits for them, and re-layouts: 70.4 us -> 33 us
    dot_general x102 -> x0, starting transfers between devices: 338 us -> none  [the longest x34 113 us: matmul(): jnp.dot(a, w, preferred_element_type=jnp.float32).astype(jnp.bfloat16)]
    reduce_scatter x0 -> x6, waiting for transfers between devices: none -> 211 us  [update(): lax.psum_scatter(term, 'dp', scatter_dimension=0, tiled=True)]
    all_gather x0 -> x6, waiting for transfers between devices: none -> 206 us  [update(): g[name, layer] = (lax.all_gather(nw, 'dp', axis=0, tiled=True), nm, nv)]
    dot_general x57 -> x15, matrix products: 456 us -> 289 us  [dot(): lax.dot_general(a, b, (dims, ((), ())), preferred_element_type=jnp.float32)]
    dot_general x96 -> x0, other arithmetic: 158 us -> none
    dot_general x102 -> x0, waiting for transfers between devices: 140 us -> none  [the longest x34 66.3 us: matmul(): jnp.dot(a, w, preferred_element_type=jnp.float32).astype(jnp.bfloat16)]
    unnamed x50 -> x36, local copies, waits for them, and re-layouts: 70.4 us -> 8.11 us
    reshape x3 -> x0, waiting for transfers between devices: 58.4 us -> none  [step(): t.reshape(-1, *t.shape[2:])]
  transfers between devices with their start and end apart: 105 -> 12, of which waited for: 65 -> 10; matrix products, arithmetic and copies ran while one was open for 40% -> 25% of each run, Pallas kernels for 0% -> 0%
where the time goes in v1:
time: 807 us; the launch traced here: 801 us
  waiting for transfers between devices  419 us (52%)
  matrix products  289 us (36%)
  other arithmetic  44.7 us (6%)
  local copies, waits for them, and re-layouts  33 us (4%)
  between operations  14.9 us (2%)
    dot_general x15, matrix products, dot(): lax.dot_general(a, b, (dims, ((), ())), preferred_element_type=jnp.float32)  289 us
    reduce_scatter x6, waiting for transfers between devices, update(): lax.psum_scatter(term, 'dp', scatter_dimension=0, tiled=True)  211 us
    all_gather x6, waiting for transfers between devices, update(): g[name, layer] = (lax.all_gather(nw, 'dp', axis=0, tiled=True), nm, nv)  206 us
    another operation x6, other arithmetic, step(): jnp.stack([g[name, 0][k], g[name, 1][k]])  31.1 us
  transfers between devices with their start and end apart: 12, of which 10 were waited for; matrix products, arithmetic and copies ran while one was open for 25% of the time, Pallas kernels for 0%

profile of v1, /device:TPU:0, one launch (start us, length us, event | category | flops | bytes accessed | tf_op | source)
XLA Modules:
  0.0 801.2 jit_solution(14043880484230599536)
XLA Ops:
  11.1 18.0 %fusion.42 = f32[2048,3072]{1,0:T(8,128)} fusion(bf16[1,2048,768]{2,1,0:T(8,128)(2,1)} %param.11, f32[2048]{0:T(1024)S(1)} %add_rsqrt_fusion.1, bf16[2,768,3072]{2,1,0:T(8,128)(2,1)} %param.13), kind=kOutput, calls=%fused_computation.60 | convolution fusion | flops 9668395008 | bytes 33038336 | tf_op jit(solution)/shard_map/dot_general | solution.py:8
  29.1 27.6 %multiply_convert_fusion.1 = (bf16[2048,3072]{1,0:T(8,128)(2,1)}, f32[2048,3072]{1,0:T(8,128)}) fusion(f32[2048,3072]{1,0:T(8,128)} %fusion.42, bf16[2,768,3072]{2,1,0:T(8,128)(2,1)} %param.14, bf16[1,2048,768]{2,1,0:T(8,128)(2,1)} %param.11, f32[2048]{0:T(1024)S(1)} %add_rsqrt_fusion.1), kind=kOutput, calls=%fused_computation.16 | convolution fusion | flops 9706143744 | bytes 70787072 | tf_op jit(solution)/shard_map/dot_general | solution.py:8
  56.7 16.3 %fusion.19 = (f32[2048]{0:T(1024)S(1)}, bf16[2048,768]{0,1:T(8,128)(2,1)}) fusion(bf16[2048,3072]{1,0:T(8,128)(2,1)} %get-tuple-element.35, bf16[2,3072,768]{2,1,0:T(8,128)(2,1)} %param.15, bf16[1,2048,768]{1,2,0:T(8,128)(2,1)S(1)} %copy.20), kind=kOutput, calls=%fused_computation.37 | convolution fusion | flops 9671538688 | bytes 23601152 | tf_op jit(solution)/shard_map/dot_general | solution.py:8
  73.1 14.9 %convolution_convert_fusion.1 = bf16[2048,3072]{1,0:T(8,128)(2,1)} fusion(bf16[1,2048,768]{2,1,0:T(8,128)(2,1)S(1)} %copy-done.2, bf16[2,3072,768]{2,1,0:T(8,128)(2,1)} %param.15), kind=kOutput, calls=%fused_computation.22 | convolution fusion | flops 9669967872 | bytes 20447232 | tf_op jit(solution)/shard_map/dot_general | solution.py:8
  88.0 15.7 %fusion.35 = f32[2048,3072]{1,0:T(8,128)} fusion(bf16[2048,768]{0,1:T(8,128)(2,1)S(1)} %copy-done.4, f32[2048]{0:T(1024)S(1)} %add_rsqrt_fusion, bf16[2,768,3072]{2,1,0:T(8,128)(2,1)} %param.14), kind=kOutput, calls=%fused_computation.53 | convolution fusion | flops 9668395008 | bytes 33038336 | tf_op jit(solution)/shard_map/dot_general | solution.py:8
  103.7 37.4 %fusion.4 = (bf16[2048,3072]{1,0:T(8,128)(2,1)}, bf16[2048,3072]{1,0:T(8,128)(2,1)}, f32[2048,3072]{1,0:T(8,128)}) fusion(bf16[2048,3072]{1,0:T(8,128)(2,1)} %convolution_convert_fusion.1, f32[2048,3072]{1,0:T(8,128)} %fusion.35, bf16[2,768,3072]{2,1,0:T(8,128)(2,1)} %param.13, bf16[2048,768]{0,1:T(8,128)(2,1)} %get-tuple-element.38, f32[2048]{0:T(1024)S(1)} %add_rsqrt_fusion), kind=kOutput, calls=%fused_computation.8 | convolution fusion | flops 9756475392 | bytes 95952896 | tf_op jit(solution)/shard_map/dot_general | solution.py:8
  141.1 22.4 %fusion.28 = bf16[3072,768]{1,0:T(8,128)(2,1)} fusion(f32[2048,3072]{1,0:T(8,128)} %fusion.35, f32[2048,3072]{1,0:T(8,128)} %get-tuple-element.39, bf16[1,2048,768]{2,1,0:T(8,128)(2,1)S(1)} %copy-done.3), kind=kOutput, calls=%fused_computation.43 | convolution fusion | flops 9703784448 | bytes 58195968 | tf_op jit(solution)/shard_map/dot_general | solution.py:8
  163.6 15.9 %fusion.48 = bf16[2048,768]{0,1:T(8,128)(2,1)} fusion(bf16[2048,3072]{1,0:T(8,128)(2,1)} %get-tuple-element.9, bf16[2,768,3072]{2,1,0:T(8,128)(2,1)} %param.14), kind=kOutput, calls=%fused_computation.64 | convolution fusion | flops 9665249280 | bytes 20447232 | tf_op jit(solution)/shard_map/dot_general | solution.py:8
  182.7 16.2 %fusion.21 = (f32[2048]{0:T(1024)S(1)}, bf16[2048,768]{0,1:T(8,128)(2,1)S(1)}) fusion(bf16[2048,768]{0,1:T(8,128)(2,1)} %get-tuple-element.38, bf16[2048,768]{0,1:T(8,128)(2,1)} %fusion.48, bf16[2048,3072]{1,0:T(8,128)(2,1)} %get-tuple-element.10, bf16[2,768,3072]{2,1,0:T(8,128)(2,1)} %param.13), kind=kOutput, calls=%fused_computation.39 | convolution fusion | flops 9673111552 | bytes 26746880 | tf_op jit(solution)/shard_map/dot_general | solution.py:8
  202.8 14.9 %convolution_convert_fusion.2 = bf16[3072,768]{1,0:T(8,128)(2,1)} fusion(bf16[2048,3072]{1,0:T(8,128)(2,1)} %get-tuple-element.35, bf16[2048,768]{0,1:T(8,128)(2,1)S(1)} %fusion.55), kind=kOutput, calls=%fused_computation.44 | convolution fusion | flops 9666035712 | bytes 20447232 | tf_op jit(solution)/shard_map/dot_general | solution.py:8
  232.2 16.0 %convolution_convert_fusion = bf16[2048,3072]{1,0:T(8,128)(2,1)} fusion(bf16[2048,768]{0,1:T(8,128)(2,1)} %copy-done.7, bf16[2,3072,768]{2,1,0:T(8,128)(2,1)} %param.15), kind=kOutput, calls=%fused_computation.21 | convolution fusion | flops 9669967872 | bytes 20447232 | tf_op jit(solution)/shard_map/dot_general | solution.py:8
  248.2 18.3 %fusion.25 = bf16[768,3072]{1,0:T(8,128)(2,1)} fusion(f32[2048,3072]{1,0:T(8,128)} %fusion.42, bf16[2048,3072]{1,0:T(8,128)(2,1)} %convolution_convert_fusion, bf16[1,2048,768]{1,2,0:T(8,128)(2,1)S(1)} %copy-done.1, f32[2048]{0:T(1024)S(1)} %copy-done.16), kind=kOutput, calls=%fused_computation.42 | convolution fusion | flops 9714794496 | bytes 45621248 | tf_op jit(solution)/shard_map/dot_general | solution.py:8
  266.6 15.5 %convolution_convert_fusion.4 = bf16[768,3072]{1,0:T(8,128)(2,1)} fusion(bf16[2048,3072]{1,0:T(8,128)(2,1)} %get-tuple-element.10, bf16[2048,768]{0,1:T(8,128)(2,1)} %get-tuple-element.38, f32[2048]{0:T(1024)S(1)} %add_rsqrt_fusion), kind=kOutput, calls=%fused_computation.46 | convolution fusion | flops 9670754304 | bytes 20455424 | tf_op jit(solution)/shard_map/dot_general | solution.py:8
  282.2 25.8 %fusion.22 = bf16[768,3072]{1,0:T(8,128)(2,1)} fusion(f32[2048,3072]{1,0:T(8,128)} %get-tuple-element.36, bf16[2048,3072]{1,0:T(8,128)(2,1)} %convolution_convert_fusion, f32[2048,3072]{1,0:T(8,128)} %fusion.42, bf16[1,2048,768]{1,2,0:T(8,128)(2,1)S(1)} %copy-done.1, f32[2048]{0:T(1024)S(1)} %copy-done.16), kind=kOutput, calls=%fused_computation.41 | convolution fusion | flops 9739960320 | bytes 70787072 | tf_op jit(solution)/shard_map/dot_general | solution.py:8
  328.5 28.7 %reduce-scatter.13.cloned.1.call-done = bf16[48,3072]{1,0:T(8,128)(2,1)} async-done(((bf16[768,3072]{1,0:T(8,128)(2,1)}), bf16[48,3072]{1,0:T(8,128)(2,1)}) %reduce-scatter.13.cloned.1.call-update) | async-done | bytes 294928 | tf_op jit(solution)/shard_map/reduce_scatter | solution.py:62
  357.2 65.3 %reduce-scatter.11.cloned.1.call-done = bf16[48,3072]{1,0:T(8,128)(2,1)} async-done(((bf16[768,3072]{1,0:T(8,128)(2,1)}), bf16[48,3072]{1,0:T(8,128)(2,1)}) %reduce-scatter.11.cloned.1.call-update) | async-done | bytes 294928 | tf_op jit(solution)/shard_map/reduce_scatter | solution.py:62
  435.5 51.6 %reduce-scatter.9.cloned.1.call-done = bf16[48,3072]{1,0:T(8,128)(2,1)} async-done(((bf16[768,3072]{1,0:T(8,128)(2,1)}), bf16[48,3072]{1,0:T(8,128)(2,1)}) %reduce-scatter.9.cloned.1.call-update) | async-done | bytes 294928 | tf_op jit(solution)/shard_map/reduce_scatter | solution.py:62
  487.1 65.3 %reduce-scatter.7.cloned.1.call-done = bf16[48,3072]{1,0:T(8,128)(2,1)} async-done(((bf16[768,3072]{1,0:T(8,128)(2,1)}), bf16[48,3072]{1,0:T(8,128)(2,1)}) %reduce-scatter.7.cloned.1.call-update) | async-done | bytes 294928 | tf_op jit(solution)/shard_map/reduce_scatter | solution.py:62
  562.8 28.4 %all-gather.15.cloned.1.call-done = bf16[3072,768]{1,0:T(8,128)(2,1)} async-done(((bf16[192,768]{1,0:T(8,128)(2,1)}), bf16[3072,768]{1,0:T(8,128)(2,1)}) %all-gather.15.cloned.1.call-update) | async-done | bytes 4718608 | tf_op jit(solution)/shard_map/all_gather | solution.py:66
  591.3 38.9 %all-gather.17.cloned.1.call-done = bf16[3072,768]{1,0:T(8,128)(2,1)} async-done(((bf16[192,768]{1,0:T(8,128)(2,1)}), bf16[3072,768]{1,0:T(8,128)(2,1)}) %all-gather.17.cloned.1.call-update) | async-done | bytes 4718608 | tf_op jit(solution)/shard_map/all_gather | solution.py:66
  638.5 30.5 %all-gather.11.cloned.1.call-done = bf16[768,3072]{1,0:T(8,128)(2,1)} async-done(((bf16[48,3072]{1,0:T(8,128)(2,1)}), bf16[768,3072]{1,0:T(8,128)(2,1)}) %all-gather.11.cloned.1.call-update) | async-done | bytes 4718608 | tf_op jit(solution)/shard_map/all_gather | solution.py:66
  669.1 38.7 %all-gather.13.cloned.1.call-done = bf16[768,3072]{1,0:T(8,128)(2,1)} async-done(((bf16[48,3072]{1,0:T(8,128)(2,1)}), bf16[768,3072]{1,0:T(8,128)(2,1)}) %all-gather.13.cloned.1.call-update) | async-done | bytes 4718608 | tf_op jit(solution)/shard_map/all_gather | solution.py:66
  716.2 30.5 %all-gather.7.cloned.1.call-done = bf16[768,3072]{1,0:T(8,128)(2,1)} async-done(((bf16[48,3072]{1,0:T(8,128)(2,1)}), bf16[768,3072]{1,0:T(8,128)(2,1)}) %all-gather.7.cloned.1.call-update) | async-done | bytes 4718608 | tf_op jit(solution)/shard_map/all_gather | solution.py:66
  746.7 38.8 %all-gather.9.cloned.1.call-done = bf16[768,3072]{1,0:T(8,128)(2,1)} async-done(((bf16[48,3072]{1,0:T(8,128)(2,1)}), bf16[768,3072]{1,0:T(8,128)(2,1)}) %all-gather.9.cloned.1.call-update) | async-done | bytes 4718608 | tf_op jit(solution)/shard_map/all_gather | solution.py:66
  (80 shorter events, 94.7 us)
Async XLA Ops:
  7.2 309.0 %reduce-scatter.17.cloned.1.call-start = ((), (), s32[]{:S(2)}) async-start(), calls=%async_computation.16 | async-start | bytes 5013504 | tf_op jit(solution)/shard_map/reduce_scatter | solution.py:62
  10.4 46.3 %copy-start = (bf16[1,2048,768]{1,2,0:T(8,128)(2,1)}, bf16[1,2048,768]{1,2,0:T(8,128)(2,1)S(1)}, u32[]{:S(2)}) copy-start(bf16[1,2048,768]{1,2,0:T(8,128)(2,1)S(1)} %copy.20) | copy-start | bytes 9437188
  11.1 18.0 %copy-start.15 = (f32[2048]{0:T(1024)}, f32[2048]{0:T(1024)S(1)}, u32[]{:S(2)}) copy-start(f32[2048]{0:T(1024)S(1)} %add_rsqrt_fusion.1) | copy-start | bytes 24580
  56.7 16.3 %copy-start.2 = (bf16[1,2048,768]{2,1,0:T(8,128)(2,1)S(1)}, bf16[1,2048,768]{2,1,0:T(8,128)(2,1)}, u32[]{:S(2)}) copy-start(bf16[1,2048,768]{2,1,0:T(8,128)(2,1)} %param.12) | copy-start | bytes 9437188
  73.0 15.0 %copy-start.13 = (f32[2048]{0:T(1024)}, f32[2048]{0:T(1024)S(1)}, u32[]{:S(2)}) copy-start(f32[2048]{0:T(1024)S(1)} %get-tuple-element.37) | copy-start | bytes 24580
  73.1 14.9 %copy-start.4 = (bf16[2048,768]{0,1:T(8,128)(2,1)S(1)}, bf16[2048,768]{0,1:T(8,128)(2,1)}, u32[]{:S(2)}) copy-start(bf16[2048,768]{0,1:T(8,128)(2,1)} %get-tuple-element.38) | copy-start | bytes 9437188
  103.7 37.4 %copy-start.3 = (bf16[1,2048,768]{2,1,0:T(8,128)(2,1)S(1)}, bf16[1,2048,768]{2,1,0:T(8,128)(2,1)}, u32[]{:S(2)}) copy-start(bf16[1,2048,768]{2,1,0:T(8,128)(2,1)} %param.12) | copy-start | bytes 9437188
  163.6 152.6 %reduce-scatter.15.cloned.1.call-start = ((), (), s32[]{:S(2)}) async-start(), calls=%async_computation.14 | async-start | bytes 5013504 | tf_op jit(solution)/shard_map/reduce_scatter | solution.py:62
  182.7 16.2 %copy-start.14 = (f32[2048]{0:T(1024)S(1)}, f32[2048]{0:T(1024)}, u32[]{:S(2)}) copy-start(f32[2048]{0:T(1024)} %copy-done.13) | copy-start | bytes 24580
  182.7 16.2 %copy-start.5 = (bf16[2048,768]{0,1:T(8,128)(2,1)S(1)}, bf16[2048,768]{0,1:T(8,128)(2,1)}, u32[]{:S(2)}) copy-start(bf16[2048,768]{0,1:T(8,128)(2,1)} %get-tuple-element.38) | copy-start | bytes 9437188
  202.8 14.9 %copy-start.6 = (bf16[2048,768]{0,1:T(8,128)(2,1)S(1)}, bf16[2048,768]{0,1:T(8,128)(2,1)}, u32[]{:S(2)}) copy-start(bf16[2048,768]{0,1:T(8,128)(2,1)} %get-tuple-element.38) | copy-start | bytes 9437188
  217.7 139.5 %reduce-scatter.13.cloned.1.call-start = ((), (), s32[]{:S(2)}) async-start(), calls=%async_computation.12 | async-start | bytes 5013504 | tf_op jit(solution)/shard_map/reduce_scatter | solution.py:62
  232.1 16.1 %copy-start.1 = (bf16[1,2048,768]{1,2,0:T(8,128)(2,1)S(1)}, bf16[1,2048,768]{1,2,0:T(8,128)(2,1)}, u32[]{:S(2)}) copy-start(bf16[1,2048,768]{1,2,0:T(8,128)(2,1)} %copy-done) | copy-start | bytes 9437188
  232.1 16.1 %copy-start.16 = (f32[2048]{0:T(1024)S(1)}, f32[2048]{0:T(1024)}, u32[]{:S(2)}) copy-start(f32[2048]{0:T(1024)} %copy-done.15) | copy-start | bytes 24580
  232.1 190.3 %reduce-scatter.11.cloned.1.call-start = ((), (), s32[]{:S(2)}) async-start(), calls=%async_computation.10 | async-start | bytes 5013504 | tf_op jit(solution)/shard_map/reduce_scatter | solution.py:62
  266.5 220.6 %reduce-scatter.9.cloned.1.call-start = ((), (), s32[]{:S(2)}) async-start(), calls=%async_computation.8 | async-start | bytes 5013504 | tf_op jit(solution)/shard_map/reduce_scatter | solution.py:62
  282.1 270.2 %reduce-scatter.7.cloned.1.call-start = ((), (), s32[]{:S(2)}) async-start(), calls=%async_computation.6 | async-start | bytes 5013504 | tf_op jit(solution)/shard_map/reduce_scatter | solution.py:62
  308.0 283.3 %all-gather.15.cloned.1.call-start = ((), (), s32[]{:S(2)}) async-start(), calls=%async_computation.15 | async-start | bytes 5013504 | tf_op jit(solution)/shard_map/all_gather | solution.py:66
  308.0 8.2 %copy-start.12 = (f32[2,192,768]{2,1,0:T(8,128)S(1)}, f32[2,192,768]{2,1,0:T(8,128)}, u32[]{:S(2)}) copy-start(f32[2,192,768]{2,1,0:T(8,128)} %param.18) | copy-start | bytes 3538948
  319.3 310.9 %all-gather.17.cloned.1.call-start = ((), (), s32[]{:S(2)}) async-start(), calls=%async_computation.17 | async-start | bytes 5013504 | tf_op jit(solution)/shard_map/all_gather | solution.py:66
  320.1 349.0 %all-gather.11.cloned.1.call-start = ((), (), s32[]{:S(2)}) async-start(), calls=%async_computation.11 | async-start | bytes 5013504 | tf_op jit(solution)/shard_map/all_gather | solution.py:66
  426.2 281.6 %all-gather.13.cloned.1.call-start = ((), (), s32[]{:S(2)}) async-start(), calls=%async_computation.13 | async-start | bytes 5013504 | tf_op jit(solution)/shard_map/all_gather | solution.py:66
  426.8 320.0 %all-gather.7.cloned.1.call-start = ((), (), s32[]{:S(2)}) async-start(), calls=%async_computation.7 | async-start | bytes 5013504 | tf_op jit(solution)/shard_map/all_gather | solution.py:66
  556.2 229.3 %all-gather.9.cloned.1.call-start = ((), (), s32[]{:S(2)}) async-start(), calls=%async_computation.9 | async-start | bytes 5013504 | tf_op jit(solution)/shard_map/all_gather | solution.py:66
  (5 other events, 19.3 us)
Sparse Core Ops, SparseCore 0:
  163.7 63.2 reduce-scatter.16
  231.9 60.3 reduce-scatter.14
  296.7 60.3 reduce-scatter.12
  362.0 60.3 reduce-scatter.10
  426.7 60.3 reduce-scatter.8
  491.9 60.3 reduce-scatter.6
  554.6 36.6 all-gather.14
  593.5 36.6 all-gather.16
  632.4 36.6 all-gather.10
  671.1 36.6 all-gather.12
  710.0 36.6 all-gather.6
  748.8 36.6 all-gather.8

commit v2 on v0

v2 whole, which is shorter than its diff:
```python
import jax
import jax.numpy as jnp
from jax import lax
from jax.experimental import pallas as pl
from jax.experimental.pallas import tpu as pltpu
from jax.sharding import PartitionSpec as P

F32, BF16 = jnp.float32, jnp.bfloat16
MESH = pl.DeviceIdType.MESH
D, FF, TOKENS, TILE, WIDE = 768, 3072, 2048, 512, 1024
PIECES = FF // WIDE
ROWS = D // 16
CHUNKS = 18
SLOTS = 8
MIB = 2**20


def dot(a, b, dims=((1,), (0,))):
    return lax.dot_general(a, b, (dims, ((), ())), preferred_element_type=F32)


NT, TN = ((1,), (1,)), ((0,), (0,))


def scale_of(wide):
    return lax.rsqrt(jnp.mean(wide * wide, -1, keepdims=True) + 1e-6)


def back_of_hidden(gate, up, d_s):
    sig = 1 / (1 + jnp.exp(-gate))
    silu = gate * sig
    d_up = d_s * silu
    d_gate = d_s * up * (sig + silu * (1 - sig))
    return silu * up, d_gate, d_up


def adamw(w, m, v, g):
    m = 0.9 * m + 0.1 * g
    v = 0.95 * v + 0.05 * g * g
    step = m * lax.rsqrt(v + 1e-8) + 0.1 * w
    return (w - 0.02 * step).astype(BF16), m, v


def forward_kernel(x, wg, wu, wd, a_out, gate_out, up_out, s_out, h_out):
    wide = x[...].astype(F32)
    a = (wide * scale_of(wide)).astype(BF16)
    a_out[...] = a
    for c in range(PIECES):
        at = slice(c * WIDE, (c + 1) * WIDE)
        gate, up = dot(a, wg[:, at]), dot(a, wu[:, at])
        gate_out[:, at] = gate
        up_out[:, at] = up
        s_out[:, at] = (gate / (1 + jnp.exp(-gate)) * up).astype(BF16)
    h_out[...] = x[...] + dot(s_out[...], wd[...]).astype(BF16)


def turn_kernel(h, dy, wg, wu, wd, a_out, s_out, dg_out, du_out, dh_out):
    wide = h[...].astype(F32)
    scale = scale_of(wide)
    a = (wide * scale).astype(BF16)
    a_out[...] = a
    for c in range(PIECES):
        at = slice(c * WIDE, (c + 1) * WIDE)
        gate, up = dot(a, wg[:, at]), dot(a, wu[:, at])
        d_s = dot(dy[...], wd[at, :], NT).astype(BF16).astype(F32)
        s, d_gate, d_up = back_of_hidden(gate, up, d_s)
        s_out[:, at] = s.astype(BF16)
        dg_out[:, at] = d_gate.astype(BF16)
        du_out[:, at] = d_up.astype(BF16)
    d_a = dot(dg_out[...], wg[...], NT).astype(BF16) + dot(du_out[...], wu[...], NT).astype(BF16)
    d_a = d_a.astype(F32)
    along = jnp.mean(d_a * wide, -1, keepdims=True)
    dh_out[...] = dy[...] + (d_a * scale - wide * (scale * scale * scale * along)).astype(BF16)


def back_kernel(dh, gate, up, wd, dg_out, du_out):
    for c in range(PIECES):
        at = slice(c * WIDE, (c + 1) * WIDE)
        d_s = dot(dh[...], wd[at, :], NT).astype(BF16).astype(F32)
        _, d_gate, d_up = back_of_hidden(gate[:, at], up[:, at], d_s)
        dg_out[:, at] = d_gate.astype(BF16)
        du_out[:, at] = d_up.astype(BF16)


def by_tiles(kernel, ins, weights, layer, outs, flops):
    def tile(width):
        return pl.BlockSpec((TILE, width), lambda i: (i, 0))

    def whole(w):
        return pl.BlockSpec((None, *w.shape[1:]), lambda i: (layer, 0, 0), pipeline_mode=pl.Buffered(1))

    return pl.pallas_call(
        kernel,
        grid=(TOKENS // TILE,),
        in_specs=[tile(t.shape[1]) for t in ins] + [whole(w) for w in weights],
        out_specs=[tile(width) for width, _ in outs],
        out_shape=[jax.ShapeDtypeStruct((TOKENS, width), dtype) for width, dtype in outs],
        compiler_params=pltpu.CompilerParams(vmem_limit_bytes=62 * MIB),
        cost_estimate=pl.CostEstimate(flops=flops, bytes_accessed=50 * MIB, transcendentals=0),
    )(*ins, *weights)


def sum_kernel(*refs):
    (a1, a0, s1, s0, dy, dh1, dg1, du1, dg0, du0, wg, wu, wd, mg, mu, md, vg, vu, vd) = refs[:19]
    (nwg, nwu, nwd, nmg, nmu, nmd, nvg, nvu, nvd) = refs[19:28]
    (a_in, s_in, rhs, part, r0, q, r1, r2, r3, new, m_in, v_in, w_in, m_out, v_out) = refs[28:43]
    (sem_a, sem_s, sem_rhs, sem_mv, sem_mvo, sem_out, x0, x1, x2, x3, g1, g2, g3, g4) = refs[43:]

    me = lax.axis_index("dp")
    pos = [me // 8, (me // 4) % 2, (me // 2) % 2]
    core = me % 2
    mate = [me + 8 - 16 * pos[0], me + 4 - 8 * pos[1], me + 2 - 4 * pos[2]]
    twin = me + 1 - 2 * core

    barrier = pltpu.get_barrier_semaphore()
    for other in (*mate, twin):
        pl.semaphore_signal(barrier, inc=1, device_id=(0, other), device_id_type=MESH)
    pl.semaphore_wait(barrier, 4)

    def remote(src, dst, sems, index, to):
        return pltpu.make_async_remote_copy(
            src_ref=src,
            dst_ref=dst,
            send_sem=sems.at[(0, *index)],
            recv_sem=sems.at[(1, *index)],
            device_id=(0, to),
            device_id_type=MESH,
        )

    def at(chosen):
        return tuple(chosen.get(axis, slice(None)) for axis in range(3))

    def which(k):
        return 1 - k // 9, (k % 9) // 3, k % 3

    def swap0(k):
        return remote(part.at[k % 2, :, :, :, 1 - core], r0.at[k % 2], x0, (k % 2,), twin)

    def rows(r):
        return pl.ds(16 * r, 16)

    def swap1(k, r):
        a = r
        src = q.at[(k % 3, *at({a: 1 - pos[a]}), rows(r))]
        return remote(src, r1.at[k % 2, r], x1, (k % 2, r), mate[a])

    def swap2(k, r):
        a, b = r, (r + 1) % 3
        src = q.at[(k % 3, *at({a: pos[a], b: 1 - pos[b]}), rows(r))]
        return remote(src, r2.at[k % 2, r], x2, (k % 2, r), mate[b])

    def swap3(k, r):
        a, b, c = r, (r + 1) % 3, (r + 2) % 3
        src = q.at[(k % 3, *at({a: pos[a], b: pos[b], c: 1 - pos[c]}), rows(r))]
        return remote(src, r3.at[k % 2, r], x3, (k % 2, r), mate[c])

    def give(k, r, known, sems, axis):
        ref = new.at[(k % SLOTS, *at({n: pos[n] for n in known}), core, rows(r))]
        return remote(ref, ref, sems, (k % 2, r), mate[axis])

    def give1(k, r):
        return give(k, r, (0, 1, 2), g1, (r + 2) % 3)

    def give2(k, r):
        return give(k, r, (r, (r + 1) % 3), g2, (r + 1) % 3)

    def give3(k, r):
        return give(k, r, (r,), g3, r)

    def give4(k):
        ref = new.at[k % SLOTS, :, :, :, core]
        return remote(ref, ref, g4, (k % 2,), twin)

    def operand(k, act):
        layer, kind, j = which(k)
        cols = pl.ds(pl.multiple_of(j * WIDE, 128), WIDE)
        few = pl.ds(pl.multiple_of(j * 256, 128), 256)
        n = 0
        for at_layer, sources in ((1, (dg1, du1, dy)), (0, (dg0, du0, dh1))):
            for at_kind, src in enumerate(sources):

                @pl.when((layer == at_layer) & (kind == at_kind))
                def _(src=src, at_kind=at_kind):
                    if at_kind < 2:
                        act(pltpu.make_async_copy(src.at[:, cols], rhs.at[k % 2], sem_rhs.at[k % 2]))
                    else:
                        act(pltpu.make_async_copy(src.at[:, few], rhs.at[k % 2, :, pl.ds(0, 256)], sem_rhs.at[k % 2]))

    def state(k, act, back):
        layer, kind, j = which(k)
        cols = pl.ds(pl.multiple_of(j * WIDE, 128), WIDE)
        few = pl.ds(pl.multiple_of(j * 256, 128), 256)
        for at_kind, (w, m, v, nm, nv) in enumerate(((wg, mg, vg, nmg, nvg), (wu, mu, vu, nmu, nvu), (wd, md, vd, nmd, nvd))):

            @pl.when(kind == at_kind)
            def _(w=w, m=m, v=v, nm=nm, nv=nv, at_kind=at_kind):
                if at_kind < 2:
                    if back:
                        act(pltpu.make_async_copy(m_out, nm.at[layer, :, cols], sem_mvo.at[0, 0]))
                        act(pltpu.make_async_copy(v_out, nv.at[layer, :, cols], sem_mvo.at[1, 0]))
                    else:
                        act(pltpu.make_async_copy(m.at[layer, :, cols], m_in, sem_mv.at[0, 0]))
                        act(pltpu.make_async_copy(v.at[layer, :, cols], v_in, sem_mv.at[1, 0]))
                        act(pltpu.make_async_copy(w.at[layer, me, :, cols], w_in, sem_mv.at[2, 0]))
                else:
                    for n in range(4):
                        here = pl.ds(256 * n, 256)
                        if back:
                            act(pltpu.make_async_copy(m_out.at[:, here], nm.at[layer, n, :, few], sem_mvo.at[0, n]))
                            act(pltpu.make_async_copy(v_out.at[:, here], nv.at[layer, n, :, few], sem_mvo.at[1, n]))
                        else:
                            act(pltpu.make_async_copy(m.at[layer, n, :, few], m_in.at[:, here], sem_mv.at[0, n]))
                            act(pltpu.make_async_copy(v.at[layer, n, :, few], v_in.at[:, here], sem_mv.at[1, n]))
                            act(pltpu.make_async_copy(w.at[layer, me, n, :, few], w_in.at[:, here], sem_mv.at[2, n]))

    def result(k, act):
        layer, kind, j = which(k)
        cols = pl.ds(pl.multiple_of(j * WIDE, 128), WIDE)
        few = pl.ds(pl.multiple_of(j * 256, 128), 256)
        for at_kind, out in enumerate((nwg, nwu, nwd)):

            @pl.when(kind == at_kind)
            def _(out=out, at_kind=at_kind):
                if at_kind < 2:
                    act(pltpu.make_async_copy(new.at[k % SLOTS], out.at[layer, :, :, :, :, :, cols], sem_out.at[k % 2, 0]))
                else:
                    for n in range(4):
                        src = new.at[k % SLOTS, :, :, :, :, :, pl.ds(256 * n, 256)]
                        act(pltpu.make_async_copy(src, out.at[layer, :, :, :, :, n, :, few], sem_out.at[k % 2, n]))

    def start(copy):
        copy.start()

    def wait(copy):
        copy.wait()

    def load_a(src):
        return pltpu.make_async_copy(src, a_in, sem_a.at[0])

    def load_s(src):
        return pltpu.make_async_copy(src, s_in, sem_s.at[0])

    load_a(a1).start()
    operand(0, start)
    load_s(s1).start()

    def step(i, carry):
        slot = i % 2

        @pl.when(i < CHUNKS)
        def _():
            operand(i, wait)

            @pl.when(i + 1 < CHUNKS)
            def _():
                operand(i + 1, start)

            @pl.when(i == 0)
            def _():
                load_a(a1).wait()

            @pl.when(i == 6)
            def _():
                load_a(a0).start()
                load_s(s1).wait()

            @pl.when(i == 9)
            def _():
                load_a(a0).wait()
                load_s(s0).start()

            @pl.when(i == 15)
            def _():
                load_s(s0).wait()

            kind = (i % 9) // 3

            @pl.when(kind < 2)
            def _():
                term = dot(a_in[...], rhs[slot], TN).astype(BF16)
                part[slot] = term.reshape(2, 2, 2, 2, ROWS, WIDE)

            @pl.when(kind == 2)
            def _():
                term = dot(s_in[...], rhs[slot, :, :256], TN).astype(BF16)
                term = term.reshape(2, 2, 2, 2, 4, ROWS, 256)
                for n in range(4):
                    part[slot, :, :, :, :, :, pl.ds(256 * n, 256)] = term[:, :, :, :, n]

        def stage(back, body):
            @pl.when((i >= back) & (i < CHUNKS + back))
            def _():
                body(i - back)

        @stage_with(stage, 9)
        def _(k):
            result(k, wait)

        @stage_with(stage, 8)
        def _(k):
            give4(k).wait()
            result(k, start)

        @stage_with(stage, 7)
        def _(k):
            for r in range(3):
                give3(k, r).wait()
            give4(k).start()

        @stage_with(stage, 6)
        def _(k):
            for r in range(3):
                give2(k, r).wait()
                give3(k, r).start()

        @stage_with(stage, 5)
        def _(k):
            state(k, wait, True)
            for r in range(3):
                give1(k, r).wait()
                give2(k, r).start()

        @stage_with(stage, 4)
        def _(k):
            state(k, wait, False)
            for r in range(3):
                swap3(k, r).wait()
                mine = (k % 3, *pos, rows(r))
                total = (q[mine].astype(F32) + r3[k % 2, r].astype(F32)).astype(BF16).astype(F32)
                w, m, v = adamw(w_in[rows(r), :].astype(F32), m_in[rows(r), :], v_in[rows(r), :], total)
                m_out[rows(r), :] = m
                v_out[rows(r), :] = v
                new[(k % SLOTS, *pos, core, rows(r))] = w
            for r in range(3):
                give1(k, r).start()
            state(k, start, True)

        @stage_with(stage, 3)
        def _(k):
            state(k, start, False)
            for r in range(3):
                a, b = r, (r + 1) % 3
                swap2(k, r).wait()
                mine = (k % 3, *at({a: pos[a], b: pos[b]}), rows(r))
                q[mine] = (q[mine].astype(F32) + r2[k % 2, r].astype(F32)).astype(BF16)
            for r in range(3):
                swap3(k, r).start()

        @stage_with(stage, 2)
        def _(k):
            for r in range(3):
                swap1(k, r).wait()
                mine = (k % 3, *at({r: pos[r]}), rows(r))
                q[mine] = (q[mine].astype(F32) + r1[k % 2, r].astype(F32)).astype(BF16)
            for r in range(3):
                swap2(k, r).start()

        @stage_with(stage, 1)
        def _(k):
            swap0(k).wait()
            for n in range(2):
                mine = part[k % 2, n, :, :, core].astype(F32) + r0[k % 2, n].astype(F32)
                q[k % 3, n] = mine.astype(BF16)
            for r in range(3):
                swap1(k, r).start()

        @pl.when(i < CHUNKS)
        def _():
            swap0(i).start()

        return carry

    lax.fori_loop(0, CHUNKS + 10, step, 0)


def stage_with(stage, back):
    return lambda body: stage(back, body)


def sum_and_step(ins, wg, wu, wd, mg, mu, md, vg, vu, vd):
    dims = (2, 2, 2, 2, 2)
    any_ = pl.BlockSpec(memory_space=pl.ANY)
    wg, wu = (w.reshape(2, 16, ROWS, FF) for w in (wg, wu))
    wd = wd.reshape(2, 16, 4, ROWS, D)
    md, vd = (t.reshape(2, 4, ROWS, D) for t in (md, vd))
    vmem = pltpu.VMEM
    dma = pltpu.SemaphoreType.DMA
    outs = pl.pallas_call(
        sum_kernel,
        in_specs=[any_] * 19,
        out_specs=[any_] * 9,
        out_shape=[jax.ShapeDtypeStruct((*dims, ROWS, FF), BF16)] * 2
        + [jax.ShapeDtypeStruct((*dims, 4, ROWS, D), BF16)]
        + ([jax.ShapeDtypeStruct((2, ROWS, FF), F32)] * 2 + [jax.ShapeDtypeStruct((2, 4, ROWS, D), F32)]) * 2,
        scratch_shapes=[
            vmem((TOKENS, D), BF16),
            vmem((TOKENS, FF), BF16),
            vmem((2, TOKENS, WIDE), BF16),
            vmem((2, 2, 2, 2, 2, ROWS, WIDE), BF16),
            vmem((2, 2, 2, 2, ROWS, WIDE), BF16),
            vmem((3, 2, 2, 2, ROWS, WIDE), BF16),
            vmem((2, 3, 2, 2, 16, WIDE), BF16),
            vmem((2, 3, 2, 16, WIDE), BF16),
            vmem((2, 3, 16, WIDE), BF16),
            vmem((SLOTS, 2, 2, 2, 2, ROWS, WIDE), BF16),
            vmem((ROWS, WIDE), F32),
            vmem((ROWS, WIDE), F32),
            vmem((ROWS, WIDE), BF16),
            vmem((ROWS, WIDE), F32),
            vmem((ROWS, WIDE), F32),
            dma((1,)),
            dma((1,)),
            dma((2,)),
            dma((3, 4)),
            dma((2, 4)),
            dma((2, 4)),
            dma((2, 2)),
            dma((2, 2, 3)),
            dma((2, 2, 3)),
            dma((2, 2, 3)),
            dma((2, 2, 3)),
            dma((2, 2, 3)),
            dma((2, 2, 3)),
            dma((2, 2)),
        ],
        compiler_params=pltpu.CompilerParams(collective_id=0, has_side_effects=True, vmem_limit_bytes=62 * MIB),
        cost_estimate=pl.CostEstimate(flops=6 * 2 * TOKENS * D * FF, bytes_accessed=120 * MIB, transcendentals=0),
    )(*ins, wg, wu, wd, mg, mu, md, vg, vu, vd)
    shapes = [(2, D, FF)] * 2 + [(2, FF, D)] + ([(2, ROWS, FF)] * 2 + [(2, 4 * ROWS, D)]) * 2
    return tuple(t.reshape(shape) for t, shape in zip(outs, shapes, strict=True))


def solution(mesh):
    def step(x, dy, wg, wu, wd, *moments):
        x, dy = x[0], dy[0]
        one = 2 * TOKENS * D * FF
        a0, gate0, up0, s0, h1 = by_tiles(
            forward_kernel, (x,), (wg, wu, wd), 0, ((D, BF16), (FF, F32), (FF, F32), (FF, BF16), (D, BF16)), 3 * one
        )
        a1, s1, dg1, du1, dh1 = by_tiles(
            turn_kernel, (h1, dy), (wg, wu, wd), 1, ((D, BF16), (FF, BF16), (FF, BF16), (FF, BF16), (D, BF16)), 5 * one
        )
        dg0, du0 = by_tiles(back_kernel, (dh1, gate0, up0), (wd,), 0, ((FF, BF16), (FF, BF16)), one)
        return sum_and_step((a1, a0, s1, s0, dy, dh1, dg1, du1, dg0, du0), wg, wu, wd, *moments)

    whole, rows = P(None, None, None), P(None, "dp", None)
    return jax.shard_map(
        step,
        mesh=mesh,
        in_specs=(P(("rep", "dp")), P(("rep", "dp")), *[whole] * 3, *[rows] * 6),
        out_specs=(*[P("rep", None, None)] * 3, *[P("rep", "dp", None)] * 6),
        check_vma=False,
    )
```

time: 1290 us -> 375 us (0.29)
  matrix products: 456 us -> 0 us
  Pallas kernels: 0 us -> 343 us
  starting transfers between devices: 338 us -> 0 us
  other arithmetic: 202 us -> 0 us
  waiting for transfers between devices: 199 us -> 0 us
  local copies, waits for them, and re-layouts: 70.4 us -> 30.8 us
  between operations: 14.5 us -> 0.66 us
    dot_general x57 -> x0, matrix products: 456 us -> none  [the longest x19 173 us: layer(): gate = jnp.dot(a, w['w_gate'], preferred_element_type=jnp.float32)]
    pallas_call x0 -> x4, Pallas kernels: none -> 343 us  [the longest x1 204 us: sum_and_step(): pl.pallas_call(sum_kernel, in_specs=[any_] * 19, out_specs=[any_] * 9, ou...]
    dot_general x102 -> x0, starting transfers between devices: 338 us -> none  [the longest x34 113 us: matmul(): jnp.dot(a, w, preferred_element_type=jnp.float32).astype(jnp.bfloat16)]
    dot_general x96 -> x0, other arithmetic: 158 us -> none
    dot_general x102 -> x0, waiting for transfers between devices: 140 us -> none  [the longest x34 66.3 us: matmul(): jnp.dot(a, w, preferred_element_type=jnp.float32).astype(jnp.bfloat16)]
    reshape x3 -> x0, waiting for transfers between devices: 58.4 us -> none  [step(): t.reshape(-1, *t.shape[2:])]
    unnamed x50 -> x21, local copies, waits for them, and re-layouts: 70.4 us -> 30.8 us
    convert_element_type x3 -> x0, other arithmetic: 23.3 us -> none  [the longest x1 21.7 us: layer(): (jax.nn.silu(gate) * up).astype(jnp.bfloat16)]
  transfers between devices with their start and end apart: 105 -> 0, of which waited for: 65 -> 0; matrix products, arithmetic and copies ran while one was open for 40% -> 0% of each run, Pallas kernels for 0% -> 0%
where the time goes in v2:
time: 375 us; the launch traced here: 374 us
  Pallas kernels  343 us (91%)
  local copies, waits for them, and re-layouts  30.8 us (8%)
    pallas_call x1, Pallas kernels, sum_and_step(): pl.pallas_call(sum_kernel, in_specs=[any_] * 19, out_specs=[any_] * 9, ou...  204 us
    pallas_call x3, Pallas kernels, by_tiles(): pl.pallas_call(kernel, grid=(TOKENS // TILE,), in_specs=[tile(t.shape[1])...  139 us
    unnamed x21, local copies, waits for them, and re-layouts  30.8 us

profile of v2, /device:TPU:0, one launch (start us, length us, event | category | flops | bytes accessed | tf_op | source)
XLA Modules:
  0.0 374.5 jit_solution(16721767719385324791)
XLA Ops:
  0.6 41.5 %shard_map.178 = (bf16[2048,768]{1,0:T(8,128)(2,1)}, f32[2048,3072]{1,0:T(8,128)}, f32[2048,3072]{1,0:T(8,128)}, bf16[2048,3072]{1,0:T(8,128)(2,1)}, bf16[2048,768]{1,0:T(8,128)(2,1)}) custom-call(bf16[2048,768]{1,0:T(8,128)(2,1)} %bitcast.20, bf16[2,768,3072]{2,1,0:T(8,128)(2,1)} %wg.3, bf16[2,768,3072]{2,1,0:T(8,128)(2,1)} %wu.3, bf16[2,3072,768]{2,1,0:T(8,128)(2,1)} %wd.5), custom_call_target="tpu_custom_call" | custom-call | flops 28991029248 | bytes 52428800 | tf_op jit(solution)/shard_map/pallas_call | solution.py:92
  42.2 63.7 %shard_map.179 = (bf16[2048,768]{1,0:T(8,128)(2,1)}, bf16[2048,3072]{1,0:T(8,128)(2,1)}, bf16[2048,3072]{1,0:T(8,128)(2,1)}, bf16[2048,3072]{1,0:T(8,128)(2,1)}, bf16[2048,768]{1,0:T(8,128)(2,1)}) custom-call(bf16[2048,768]{1,0:T(8,128)(2,1)} %get-tuple-element.30.h, bf16[2048,768]{1,0:T(8,128)(2,1)} %bitcast.21, bf16[2,768,3072]{2,1,0:T(8,128)(2,1)} %wg.3, ...), custom_call_target="tpu_custom_call" | custom-call | flops 48318382080 | bytes 52428800 | tf_op jit(solution)/shard_map/pallas_call | solution.py:92
  105.8 33.4 %shard_map.180 = (bf16[2048,3072]{1,0:T(8,128)(2,1)}, bf16[2048,3072]{1,0:T(8,128)(2,1)}) custom-call(bf16[2048,768]{1,0:T(8,128)(2,1)} %get-tuple-element.35.dh.refs_5_, f32[2048,3072]{1,0:T(8,128)} %get-tuple-element.38.gate, f32[2048,3072]{1,0:T(8,128)} %get-tuple-element.39.up, bf16[2,3072,768]{2,1,0:T(8,128)(2,1)} %wd.5), custom_call_target="tpu_custom_call" | custom-call | flops 9663676416 | bytes 52428800 | tf_op jit(solution)/shard_map/pallas_call | solution.py:92
  139.3 204.4 %shard_map.181 = (bf16[2,2,2,2,2,48,3072]{6,5,4,3,2,1,0:T(8,128)(2,1)}, bf16[2,2,2,2,2,48,3072]{6,5,4,3,2,1,0:T(8,128)(2,1)}, bf16[2,2,2,2,2,4,48,768]{7,6,5,4,3...) custom-call(bf16[2048,768]{1,0:T(8,128)(2,1)} %get-tuple-element.31., ...), custom_call_target="tpu_custom_call" | custom-call | flops 57982058496 | bytes 125829120 | tf_op jit(solution)/shard_map/pallas_call | solution.py:388
  343.6 8.3 %copy.29 = bf16[2,768,3072]{2,1,0:T(8,128)(2,1)} copy(bf16[2,768,3072]{2,1,0:T(8,128)(2,1)} %bitcast.14) | data formatting | bytes 18874368
  351.9 8.3 %copy.30 = bf16[2,768,3072]{2,1,0:T(8,128)(2,1)} copy(bf16[2,768,3072]{2,1,0:T(8,128)(2,1)} %bitcast.13) | data formatting | bytes 18874368
  360.2 0.0 copy-start.5
  360.2 0.0 copy-start.4
  360.2 8.2 %copy.31 = bf16[2,3072,768]{2,1,0:T(8,128)(2,1)} copy(bf16[2,3072,768]{2,1,0:T(8,128)(2,1)} %bitcast.12) | data formatting | bytes 18874368
  368.4 0.0 copy-done.5
  368.4 0.0 copy-start.3
  368.4 0.0 copy-start.2
  368.4 1.0 copy.32
  369.4 0.0 copy-done.4
  369.4 0.0 copy-start.1
  369.4 1.0 copy.33
  370.4 0.0 copy-done.3
  370.4 1.0 copy.34
  371.4 0.0 copy-done.2
  371.4 1.0 copy.35
  372.4 0.0 copy-done.1
  372.4 1.0 copy.36
  373.5 0.0 copy-done
  373.5 1.0 copy.37
  (1 shorter events, 0.0 us)
Async XLA Ops:
  360.2 8.2 %copy-start.5 = (f32[2,48,3072]{2,1,0:T(8,128)S(1)}, f32[2,48,3072]{2,1,0:T(8,128)}, u32[]{:S(2)}) copy-start(f32[2,48,3072]{2,1,0:T(8,128)} %get-tuple-element.63) | copy-start | bytes 3538948
  360.2 9.2 %copy-start.4 = (f32[2,48,3072]{2,1,0:T(8,128)S(1)}, f32[2,48,3072]{2,1,0:T(8,128)}, u32[]{:S(2)}) copy-start(f32[2,48,3072]{2,1,0:T(8,128)} %get-tuple-element.64) | copy-start | bytes 3538948
  368.4 2.0 copy-start.3
  368.4 3.1 copy-start.2
  369.4 3.1 copy-start.1
  370.4 3.1 copy-start

commit v3 on v2

v3 whole, which is shorter than its diff:
```python
import jax
import jax.numpy as jnp
from jax import lax
from jax.experimental import pallas as pl
from jax.experimental.pallas import tpu as pltpu
from jax.sharding import PartitionSpec as P

F32, BF16 = jnp.float32, jnp.bfloat16
MESH = pl.DeviceIdType.MESH
D, FF, TOKENS, TILE, WIDE = 768, 3072, 2048, 512, 1024
PIECES = FF // WIDE
ROWS = D // 16
CHUNKS = 18
SMALL, NARROW = 256, 512
SIXTHS = FF // NARROW
AHEAD = 4
COPIES = 3
MIB = 2**20


def dot(a, b, dims=((1,), (0,))):
    return lax.dot_general(a, b, (dims, ((), ())), preferred_element_type=F32)


NT, TN = ((1,), (1,)), ((0,), (0,))


def scale_of(wide):
    return lax.rsqrt(jnp.mean(wide * wide, -1, keepdims=True) + 1e-6)


def silu_and_slope(gate):
    sig = 0.5 * jnp.tanh(0.5 * gate) + 0.5
    silu = gate * sig
    return silu, 0.5 * (sig + silu * (1 - sig))


def adamw(w, m, v, g):
    m = 0.9 * m + 0.1 * g
    v = 0.95 * v + 0.05 * g * g
    step = m * lax.rsqrt(v + 1e-8) + 0.1 * w
    return (w - 0.02 * step).astype(BF16), m, v


def forward_kernel(x, wg, wu, wd, a_out, silu_out, slope_out, s_out, h_out):
    wide = x[...].astype(F32)
    a = (wide * scale_of(wide)).astype(BF16)
    a_out[...] = a
    for c in range(PIECES):
        at = slice(c * WIDE, (c + 1) * WIDE)
        gate, up = dot(a, wg[:, at]), dot(a, wu[:, at])
        silu, slope = silu_and_slope(gate)
        silu_out[:, at] = silu
        slope_out[:, at] = up * slope
        s_out[:, at] = (silu * up).astype(BF16)
    h_out[...] = x[...] + dot(s_out[...], wd[...]).astype(BF16)


def turn_kernel(h, dy, wg, wu, wd, a_out, s_out, dg_out, du_out):
    wide = h[...].astype(F32)
    a = (wide * scale_of(wide)).astype(BF16)
    a_out[...] = a
    for c in range(PIECES):
        at = slice(c * WIDE, (c + 1) * WIDE)
        gate, up = dot(a, wg[:, at]), dot(a, wu[:, at])
        d_s = dot(dy[...], wd[at, :], NT).astype(BF16).astype(F32)
        silu, slope = silu_and_slope(gate)
        s_out[:, at] = (silu * up).astype(BF16)
        dg_out[:, at] = (d_s * (up * slope) * 2).astype(BF16)
        du_out[:, at] = (d_s * silu).astype(BF16)


def by_tiles(kernel, ins, weights, layer, outs, flops):
    def tile(width):
        return pl.BlockSpec((TILE, width), lambda i: (i, 0))

    def whole(w):
        return pl.BlockSpec((None, *w.shape[1:]), lambda i: (layer, 0, 0), pipeline_mode=pl.Buffered(1))

    return pl.pallas_call(
        kernel,
        grid=(TOKENS // TILE,),
        in_specs=[tile(t.shape[1]) for t in ins] + [whole(w) for w in weights],
        out_specs=[tile(width) for width, _ in outs],
        out_shape=[jax.ShapeDtypeStruct((TOKENS, width), dtype) for width, dtype in outs],
        compiler_params=pltpu.CompilerParams(vmem_limit_bytes=62 * MIB),
        cost_estimate=pl.CostEstimate(flops=flops, bytes_accessed=50 * MIB, transcendentals=0),
    )(*ins, *weights)


def sum_kernel(*refs):
    (a1, a0, s1, s0, dy, h1, dg1, du1, silu0, slope0, wg, wu, wd, mg, mu, md, vg, vu, vd) = refs[:19]
    (nwg, nwu, nwd, nmg, nmu, nmd, nvg, nvu, nvd, dg0, du0) = refs[19:30]
    (a_in, s_in, rhs, part, r0, q, r1, r2, r3, new, new_d, m_in, v_in, w_in, m_out, v_out) = refs[30:46]
    (wg_in, wu_in, wd_in, dh, d_tile, h_tile, kept) = refs[46:53]
    (sem_a, sem_s, sem_rhs, sem_mv, sem_mvo, sem_own, x0, x1, x2, x3, g1, g2, g3, g4, sem_w, sem_tile, sem_kept, sem_d) = refs[53:]

    me = lax.axis_index("dp")
    pos = [me // 8, (me // 4) % 2, (me // 2) % 2]
    core = me % 2
    mate = [me + 8 - 16 * pos[0], me + 4 - 8 * pos[1], me + 2 - 4 * pos[2]]
    twin = me + 1 - 2 * core

    barrier = pltpu.get_barrier_semaphore()
    for other in (*mate, twin):
        pl.semaphore_signal(barrier, inc=1, device_id=(0, other), device_id_type=MESH)
    pl.semaphore_wait(barrier, 4)

    def remote(src, dst, sems, index, to):
        return pltpu.make_async_remote_copy(
            src_ref=src,
            dst_ref=dst,
            send_sem=sems.at[(0, *index)],
            recv_sem=sems.at[(1, *index)],
            device_id=(0, to),
            device_id_type=MESH,
        )

    def at(chosen):
        return tuple(chosen.get(axis, slice(None)) for axis in range(3))

    def which(k):
        layer, third = 1 - k // 9, k // 3
        return layer, layer * ((2 * third) % 3) + (1 - layer) * ((third + 2) % 3), k % 3

    def swap0(k):
        return remote(part.at[k % 2, :, :, :, 1 - core], r0.at[k % 2], x0, (k % 2,), twin)

    def rows(r):
        return pl.ds(16 * r, 16)

    def swap1(k, r):
        a = r
        src = q.at[(k % 3, *at({a: 1 - pos[a]}), rows(r))]
        return remote(src, r1.at[k % 2, r], x1, (k % 2, r), mate[a])

    def swap2(k, r):
        a, b = r, (r + 1) % 3
        src = q.at[(k % 3, *at({a: pos[a], b: 1 - pos[b]}), rows(r))]
        return remote(src, r2.at[k % 2, r], x2, (k % 2, r), mate[b])

    def swap3(k, r):
        a, b, c = r, (r + 1) % 3, (r + 2) % 3
        src = q.at[(k % 3, *at({a: pos[a], b: pos[b], c: 1 - pos[c]}), rows(r))]
        return remote(src, r3.at[k % 2, r], x3, (k % 2, r), mate[c])

    def by_kind(k, gate_like, down_like):
        layer, kind, j = which(k)
        cols = pl.ds(pl.multiple_of(j * WIDE, 128), WIDE)
        few = pl.ds(pl.multiple_of(j * 256, 128), 256)

        @pl.when(kind == 0)
        def _():
            gate_like(nwg, layer, cols)

        @pl.when(kind == 1)
        def _():
            gate_like(nwu, layer, cols)

        @pl.when(kind == 2)
        def _():
            down_like(nwd, layer, few)

    def give1(k, act):
        def send(r, src, dst):
            act(remote(src, dst, g1, (k % 2, r), mate[(r + 2) % 3]))

        def gate_like(out, layer, cols):
            act(pltpu.make_async_copy(new, out.at[(layer, *pos, core, slice(None), cols)], sem_own.at[0]))
            for r in range(3):
                send(r, new.at[rows(r), :], out.at[(layer, *pos, core, rows(r), cols)])

        def down_like(out, layer, few):
            act(pltpu.make_async_copy(new_d, out.at[(layer, *pos, core, slice(None), slice(None), few)], sem_own.at[0]))
            for r in range(3):
                send(r, new_d.at[:, rows(r), :], out.at[(layer, *pos, core, slice(None), rows(r), few)])

        by_kind(k, gate_like, down_like)

    def give(k, known, sems, axis, act):
        def gate_like(out, layer, cols):
            for r in range(3):
                chips = at({(r + n) % 3: pos[(r + n) % 3] for n in range(known)})
                ref = out.at[(layer, *chips, core, rows(r), cols)]
                act(remote(ref, ref, sems, (k % 2, r), mate[(r + axis) % 3]))

        def down_like(out, layer, few):
            for r in range(3):
                chips = at({(r + n) % 3: pos[(r + n) % 3] for n in range(known)})
                ref = out.at[(layer, *chips, core, slice(None), rows(r), few)]
                act(remote(ref, ref, sems, (k % 2, r), mate[(r + axis) % 3]))

        by_kind(k, gate_like, down_like)

    def give2(k, act):
        give(k, 2, g2, 1, act)

    def give3(k, act):
        give(k, 1, g3, 0, act)

    def give4(k, act):
        def gate_like(out, layer, cols):
            ref = out.at[layer, :, :, :, core, :, cols]
            act(remote(ref, ref, g4, (k % 2,), twin))

        def down_like(out, layer, few):
            ref = out.at[layer, :, :, :, core, :, :, few]
            act(remote(ref, ref, g4, (k % 2,), twin))

        by_kind(k, gate_like, down_like)

    def operand(k, act):
        layer, kind, j = which(k)
        cols = pl.ds(pl.multiple_of(j * WIDE, 128), WIDE)
        few = pl.ds(pl.multiple_of(j * 256, 128), 256)
        n = 0
        for at_layer, sources in ((1, (dg1, du1, dy)), (0, (dg0, du0, dh))):
            for at_kind, src in enumerate(sources):

                @pl.when((layer == at_layer) & (kind == at_kind))
                def _(src=src, at_kind=at_kind):
                    if at_kind < 2:
                        act(pltpu.make_async_copy(src.at[:, cols], rhs.at[k % 2], sem_rhs.at[k % 2]))
                    else:
                        act(pltpu.make_async_copy(src.at[:, few], rhs.at[k % 2, :, pl.ds(0, 256)], sem_rhs.at[k % 2]))

    def state(k, act, back):
        layer, kind, j = which(k)
        cols = pl.ds(pl.multiple_of(j * WIDE, 128), WIDE)
        few = pl.ds(pl.multiple_of(j * 256, 128), 256)
        for at_kind, (w, m, v, nm, nv) in enumerate(((wg, mg, vg, nmg, nvg), (wu, mu, vu, nmu, nvu), (wd, md, vd, nmd, nvd))):

            @pl.when(kind == at_kind)
            def _(w=w, m=m, v=v, nm=nm, nv=nv, at_kind=at_kind):
                if at_kind < 2:
                    if back:
                        act(pltpu.make_async_copy(m_out, nm.at[layer, :, cols], sem_mvo.at[0, 0]))
                        act(pltpu.make_async_copy(v_out, nv.at[layer, :, cols], sem_mvo.at[1, 0]))
                    else:
                        act(pltpu.make_async_copy(m.at[layer, :, cols], m_in, sem_mv.at[0, 0]))
                        act(pltpu.make_async_copy(v.at[layer, :, cols], v_in, sem_mv.at[1, 0]))
                        act(pltpu.make_async_copy(w.at[layer, pl.ds(pl.multiple_of(me * ROWS, 16), ROWS), cols], w_in, sem_mv.at[2, 0]))
                else:
                    for n in range(4):
                        here = pl.ds(256 * n, 256)
                        if back:
                            act(pltpu.make_async_copy(m_out.at[:, here], nm.at[layer, n, :, few], sem_mvo.at[0, n]))
                            act(pltpu.make_async_copy(v_out.at[:, here], nv.at[layer, n, :, few], sem_mvo.at[1, n]))
                        else:
                            act(pltpu.make_async_copy(m.at[layer, n, :, few], m_in.at[:, here], sem_mv.at[0, n]))
                            act(pltpu.make_async_copy(v.at[layer, n, :, few], v_in.at[:, here], sem_mv.at[1, n]))
                            own = pl.ds(pl.multiple_of((4 * me + n) * ROWS, 16), ROWS)
                            act(pltpu.make_async_copy(w.at[layer, own, few], w_in.at[:, here], sem_mv.at[2, n]))

    def start(copy):
        copy.start()

    def wait(copy):
        copy.wait()

    def load_a(src):
        return pltpu.make_async_copy(src, a_in, sem_a.at[0])

    def load_s(src):
        return pltpu.make_async_copy(src, s_in, sem_s.at[0])

    def tile(t, act):
        here = pl.ds(pl.multiple_of(t * SMALL, SMALL), SMALL)
        for n, src in enumerate((dg1, du1)):
            act(pltpu.make_async_copy(src.at[here, :], d_tile.at[n], sem_tile.at[n]))
        for n, src in enumerate((h1, dy)):
            act(pltpu.make_async_copy(src.at[here, :], h_tile.at[n], sem_tile.at[2 + n]))

    def hidden(n, act):
        here = pl.ds(pl.multiple_of((n // SIXTHS) * SMALL, SMALL), SMALL)
        cols = pl.ds(pl.multiple_of((n % SIXTHS) * NARROW, 128), NARROW)
        for m, src in enumerate((silu0, slope0)):
            act(pltpu.make_async_copy(src.at[here, cols], kept.at[n % AHEAD, m], sem_kept.at[n % AHEAD, m]))

    def back(t, act):
        here = pl.ds(pl.multiple_of(t * SMALL, SMALL), SMALL)
        for n, out in enumerate((dg0, du0)):
            act(pltpu.make_async_copy(d_tile.at[n], out.at[here, :], sem_d.at[n]))

    def load_w(n):
        src, dst = ((wg.at[1], wg_in), (wu.at[1], wu_in), (wd.at[0], wd_in))[n]
        return pltpu.make_async_copy(src, dst, sem_w.at[n])

    load_a(a1).start()
    operand(0, start)
    tile(0, start)
    load_w(0).start()
    load_w(1).start()
    load_s(s1).start()
    load_w(2).start()
    for n in range(AHEAD):
        hidden(n, start)

    def step(i, carry):
        slot = i % 2

        @pl.when(i < CHUNKS)
        def _():
            operand(i, wait)

            @pl.when((i + 1 < CHUNKS) & (i != 11))
            def _():
                operand(i + 1, start)

            @pl.when(i == 0)
            def _():
                load_a(a1).wait()

            @pl.when(i == 3)
            def _():
                load_s(s1).wait()

            @pl.when(i == 6)
            def _():
                load_s(s0).start()

            @pl.when(i == 9)
            def _():
                load_a(a0).start()
                load_s(s0).wait()

            @pl.when(i == 12)
            def _():
                load_a(a0).wait()

            _, kind, _ = which(i)

            @pl.when(kind < 2)
            def _():
                term = dot(a_in[...], rhs[slot], TN).astype(BF16)
                part[slot] = term.reshape(2, 2, 2, 2, ROWS, WIDE)

            @pl.when(kind == 2)
            def _():
                for x in range(2):
                    term = dot(s_in[:, x * (FF // 2) : (x + 1) * (FF // 2)], rhs[slot, :, :256], TN).astype(BF16)
                    term = term.reshape(2, 2, 2, 4, ROWS, 256)
                    for n in range(4):
                        part[slot, x, :, :, :, :, pl.ds(256 * n, 256)] = term[:, :, :, n]

        @pl.when((i >= 5) & (i < 12))
        def _():
            back(i - 5, wait)

        @pl.when((i >= 1) & (i < 8))
        def _():
            tile(i, start)

        def stage(back, body):
            @pl.when((i >= back) & (i < CHUNKS + back))
            def _():
                body(i - back)

        @stage_with(stage, 8)
        def _(k):
            give4(k, wait)

        @stage_with(stage, 7)
        def _(k):
            give3(k, wait)
            give4(k, start)

        @stage_with(stage, 6)
        def _(k):
            give2(k, wait)
            give3(k, start)

        @stage_with(stage, 5)
        def _(k):
            state(k, wait, True)
            give1(k, wait)
            give2(k, start)

        @stage_with(stage, 4)
        def _(k):
            state(k, wait, False)
            for r in range(3):
                swap3(k, r).wait()
                mine = (k % 3, *pos, rows(r))
                total = (q[mine].astype(F32) + r3[k % 2, r].astype(F32)).astype(BF16).astype(F32)
                w, m, v = adamw(w_in[rows(r), :].astype(F32), m_in[rows(r), :], v_in[rows(r), :], total)
                m_out[rows(r), :] = m
                v_out[rows(r), :] = v
                new[rows(r), :] = w
                for n in range(4):
                    new_d[n, rows(r), :] = w[:, 256 * n : 256 * n + 256]
            give1(k, start)
            state(k, start, True)

        @stage_with(stage, 3)
        def _(k):
            state(k, start, False)
            for r in range(3):
                a, b = r, (r + 1) % 3
                swap2(k, r).wait()
                mine = (k % 3, *at({a: pos[a], b: pos[b]}), rows(r))
                q[mine] = (q[mine].astype(F32) + r2[k % 2, r].astype(F32)).astype(BF16)
            for r in range(3):
                swap3(k, r).start()

        @stage_with(stage, 2)
        def _(k):
            for r in range(3):
                swap1(k, r).wait()
                mine = (k % 3, *at({r: pos[r]}), rows(r))
                q[mine] = (q[mine].astype(F32) + r1[k % 2, r].astype(F32)).astype(BF16)
            for r in range(3):
                swap2(k, r).start()

        @stage_with(stage, 1)
        def _(k):
            swap0(k).wait()
            for n in range(2):
                mine = part[k % 2, n, :, :, core].astype(F32) + r0[k % 2, n].astype(F32)
                q[k % 3, n] = mine.astype(BF16)
            for r in range(3):
                swap1(k, r).start()

        @pl.when(i < CHUNKS)
        def _():
            swap0(i).start()

        @pl.when(i < 8)
        def _():
            tile(i, wait)

            @pl.when(i == 0)
            def _():
                load_w(0).wait()
                load_w(1).wait()

            d_a = dot(d_tile[0], wg_in[...], NT).astype(BF16) + dot(d_tile[1], wu_in[...], NT).astype(BF16)
            d_a = d_a.astype(F32)
            wide = h_tile[0].astype(F32)
            scale = scale_of(wide)
            along = jnp.mean(d_a * wide, -1, keepdims=True)
            d_h = (d_a * scale - wide * (scale * scale * scale * along)).astype(BF16)
            dh[pl.ds(pl.multiple_of(i * SMALL, SMALL), SMALL), :] = h_tile[1] + d_h

        @pl.when((i >= 4) & (i < 12))
        def _():
            @pl.when(i == 4)
            def _():
                load_w(2).wait()

            t = i - 4
            here = pl.ds(pl.multiple_of(t * SMALL, SMALL), SMALL)
            for p in range(SIXTHS):
                n = SIXTHS * t + p
                cols = slice(p * NARROW, (p + 1) * NARROW)
                hidden(n, wait)
                d_s = dot(dh[here, :], wd_in[cols, :], NT).astype(BF16).astype(F32)
                d_tile[0, :, cols] = (d_s * kept[n % AHEAD, 1] * 2).astype(BF16)
                d_tile[1, :, cols] = (d_s * kept[n % AHEAD, 0]).astype(BF16)

                @pl.when(n + AHEAD < 8 * SIXTHS)
                def _(n=n):
                    hidden(n + AHEAD, start)

            back(t, start)

        @pl.when(i == 11)
        def _():
            back(7, wait)
            operand(12, start)

        return carry

    lax.fori_loop(0, CHUNKS + 8, step, 0)


def stage_with(stage, back):
    return lambda body: stage(back, body)


def sum_and_step(ins, wg, wu, wd, mg, mu, md, vg, vu, vd):
    dims = (2, 2, 2, 2, 2)
    any_ = pl.BlockSpec(memory_space=pl.ANY)
    md, vd = (t.reshape(2, 4, ROWS, D) for t in (md, vd))
    vmem = pltpu.VMEM
    dma = pltpu.SemaphoreType.DMA
    outs = pl.pallas_call(
        sum_kernel,
        in_specs=[any_] * 19,
        out_specs=[any_] * 11,
        out_shape=[jax.ShapeDtypeStruct((*dims, ROWS, FF), BF16)] * 2
        + [jax.ShapeDtypeStruct((*dims, 4, ROWS, D), BF16)]
        + ([jax.ShapeDtypeStruct((2, ROWS, FF), F32)] * 2 + [jax.ShapeDtypeStruct((2, 4, ROWS, D), F32)]) * 2
        + [jax.ShapeDtypeStruct((TOKENS, FF), BF16)] * 2,
        scratch_shapes=[
            vmem((TOKENS, D), BF16),
            vmem((TOKENS, FF), BF16),
            vmem((2, TOKENS, WIDE), BF16),
            vmem((2, 2, 2, 2, 2, ROWS, WIDE), BF16),
            vmem((2, 2, 2, 2, ROWS, WIDE), BF16),
            vmem((3, 2, 2, 2, ROWS, WIDE), BF16),
            vmem((2, 3, 2, 2, 16, WIDE), BF16),
            vmem((2, 3, 2, 16, WIDE), BF16),
            vmem((2, 3, 16, WIDE), BF16),
            vmem((ROWS, WIDE), BF16),
            vmem((4, ROWS, 256), BF16),
            vmem((ROWS, WIDE), F32),
            vmem((ROWS, WIDE), F32),
            vmem((ROWS, WIDE), BF16),
            vmem((ROWS, WIDE), F32),
            vmem((ROWS, WIDE), F32),
            vmem((D, FF), BF16),
            vmem((D, FF), BF16),
            vmem((FF, D), BF16),
            vmem((TOKENS, D), BF16),
            vmem((2, SMALL, FF), BF16),
            vmem((2, SMALL, D), BF16),
            vmem((AHEAD, 2, SMALL, NARROW), F32),
            dma((1,)),
            dma((1,)),
            dma((2,)),
            dma((3, 4)),
            dma((2, 4)),
            dma((1,)),
            dma((2, 2)),
            *[dma((2, 2, 3))] * 6,
            dma((2, 2)),
            dma((3,)),
            dma((4,)),
            dma((AHEAD, 2)),
            dma((2,)),
        ],
        compiler_params=pltpu.CompilerParams(collective_id=0, has_side_effects=True, vmem_limit_bytes=67043328),
        cost_estimate=pl.CostEstimate(flops=9 * 2 * TOKENS * D * FF, bytes_accessed=120 * MIB, transcendentals=0),
    )(*ins, wg, wu, wd, mg, mu, md, vg, vu, vd)
    shapes = [(2, D, FF)] * 2 + [(2, FF, D)] + ([(2, ROWS, FF)] * 2 + [(2, 4 * ROWS, D)]) * 2
    return copied([t.reshape(shape) for t, shape in zip(outs[:9], shapes, strict=True)])


def copy_kernel(*refs):
    n = len(refs) // 2
    for src, dst in zip(refs[:n], refs[n:], strict=True):
        dst[...] = src[...]


def copied(arrays):
    specs = [pl.BlockSpec((None, t.shape[1] // COPIES, t.shape[2]), lambda i: (i // COPIES, i % COPIES, 0)) for t in arrays]
    return tuple(
        pl.pallas_call(
            copy_kernel,
            grid=(2 * COPIES,),
            in_specs=specs,
            out_specs=specs,
            out_shape=[jax.ShapeDtypeStruct(t.shape, t.dtype) for t in arrays],
            compiler_params=pltpu.CompilerParams(vmem_limit_bytes=62 * MIB),
        )(*arrays)
    )


def solution(mesh):
    def step(x, dy, wg, wu, wd, *moments):
        x, dy = x[0], dy[0]
        one = 2 * TOKENS * D * FF
        a0, silu0, slope0, s0, h1 = by_tiles(
            forward_kernel, (x,), (wg, wu, wd), 0, ((D, BF16), (FF, F32), (FF, F32), (FF, BF16), (D, BF16)), 3 * one
        )
        a1, s1, dg1, du1 = by_tiles(
            turn_kernel, (h1, dy), (wg, wu, wd), 1, ((D, BF16), (FF, BF16), (FF, BF16), (FF, BF16)), 3 * one
        )
        return sum_and_step((a1, a0, s1, s0, dy, h1, dg1, du1, silu0, slope0), wg, wu, wd, *moments)

    whole, rows = P(None, None, None), P(None, "dp", None)
    return jax.shard_map(
        step,
        mesh=mesh,
        in_specs=(P(("rep", "dp")), P(("rep", "dp")), *[whole] * 3, *[rows] * 6),
        out_specs=(*[P("rep", None, None)] * 3, *[P("rep", "dp", None)] * 6),
        check_vma=False,
    )
```

time: 375 us -> 350 us (0.933)
  local copies, waits for them, and re-layouts: 30.8 us -> 0 us
  Pallas kernels: 343 us -> 349 us
    pallas_call x1 -> x2, Pallas kernels: 204 us -> 263 us  [the longest x1 240 us: sum_and_step(): pl.pallas_call(sum_kernel, in_specs=[any_] * 19, out_specs=[any_] * 11, o...]
    pallas_call x3 -> x2, Pallas kernels: 139 us -> 85.7 us  [by_tiles(): pl.pallas_call(kernel, grid=(TOKENS // TILE,), in_specs=[tile(t.shape[1])...]
    unnamed x21 -> x0, local copies, waits for them, and re-layouts: 30.8 us -> none
where the time goes in v3:
time: 350 us
  Pallas kernels  349 us (100%)
    pallas_call x1, Pallas kernels, sum_and_step(): pl.pallas_call(sum_kernel, in_specs=[any_] * 19, out_specs=[any_] * 11, o...  240 us
    pallas_call x2, Pallas kernels, by_tiles(): pl.pallas_call(kernel, grid=(TOKENS // TILE,), in_specs=[tile(t.shape[1])...  85.7 us
    pallas_call x1, Pallas kernels, copied(): pl.pallas_call(copy_kernel, grid=(2 * COPIES,), in_specs=specs, out_specs...  23 us

profile of v3, /device:TPU:0, one launch (start us, length us, event | category | flops | bytes accessed | tf_op | source)
XLA Modules:
  0.0 350.0 jit_solution(4358910247764794114)
XLA Ops:
  0.6 42.3 %shard_map.178 = (bf16[2048,768]{1,0:T(8,128)(2,1)}, f32[2048,3072]{1,0:T(8,128)}, f32[2048,3072]{1,0:T(8,128)}, bf16[2048,3072]{1,0:T(8,128)(2,1)}, bf16[2048,768]{1,0:T(8,128)(2,1)}) custom-call(bf16[2048,768]{1,0:T(8,128)(2,1)} %bitcast.14, bf16[2,768,3072]{2,1,0:T(8,128)(2,1)} %refs_10_.1, bf16[2,768,3072]{2,1,0:T(8,128)(2,1)} %refs_11_.1, ...), custom_call_target="tpu_custom_call" | custom-call | flops 28991029248 | bytes 52428800 | tf_op jit(solution)/shard_map/pallas_call | solution.py:80
  42.9 43.4 %shard_map.179 = (bf16[2048,768]{1,0:T(8,128)(2,1)}, bf16[2048,3072]{1,0:T(8,128)(2,1)}, bf16[2048,3072]{1,0:T(8,128)(2,1)}, bf16[2048,3072]{1,0:T(8,128)(2,1)}) custom-call(bf16[2048,768]{1,0:T(8,128)(2,1)} %get-tuple-element.27.h.refs_5_, bf16[2048,768]{1,0:T(8,128)(2,1)} %bitcast.15, bf16[2,768,3072]{2,1,0:T(8,128)(2,1)} %refs_10_.1, ...), custom_call_target="tpu_custom_call" | custom-call | flops 28991029248 | bytes 52428800 | tf_op jit(solution)/shard_map/pallas_call | solution.py:80
  86.4 240.4 %shard_map.180 = (bf16[2,2,2,2,2,48,3072]{6,5,4,3,2,1,0:T(8,128)(2,1)}, bf16[2,2,2,2,2,48,3072]{6,5,4,3,2,1,0:T(8,128)(2,1)}, bf16[2,2,2,2,2,4,48,768]{7,6,5,4,3...) custom-call(bf16[2048,768]{1,0:T(8,128)(2,1)} %get-tuple-element.28., ...), custom_call_target="tpu_custom_call" | custom-call | flops 86973087744 | bytes 125829120 | tf_op jit(solution)/shard_map/pallas_call | solution.py:487
  326.8 23.0 %shard_map.181 = (bf16[2,768,3072]{2,1,0:T(8,128)(2,1)}, bf16[2,768,3072]{2,1,0:T(8,128)(2,1)}, bf16[2,3072,768]{2,1,0:T(8,128)(2,1)}, f32[2,48,3072]{2,1,0:T(8,...) custom-call(bf16[2,768,3072]{2,1,0:T(8,128)(2,1)} %bitcast.9, ...), custom_call_target="tpu_custom_call" | custom-call | tf_op jit(solution)/shard_map/pallas_call | solution.py:549

commit v4 on v3

--- a/solution.py
+++ b/solution.py
@@ -8,7 +8,6 @@
 F32, BF16 = jnp.float32, jnp.bfloat16
 MESH = pl.DeviceIdType.MESH
 D, FF, TOKENS, TILE, WIDE = 768, 3072, 2048, 512, 1024
-PIECES = FF // WIDE
 ROWS = D // 16
 CHUNKS = 18
 SMALL, NARROW = 256, 512
@@ -42,49 +41,66 @@
     return (w - 0.02 * step).astype(BF16), m, v
 
 
-def forward_kernel(x, wg, wu, wd, a_out, silu_out, slope_out, s_out, h_out):
-    wide = x[...].astype(F32)
-    a = (wide * scale_of(wide)).astype(BF16)
-    a_out[...] = a
-    for c in range(PIECES):
-        at = slice(c * WIDE, (c + 1) * WIDE)
-        gate, up = dot(a, wg[:, at]), dot(a, wu[:, at])
+def forward_kernel(x, wg, wu, wd, a_out, silu_out, slope_out, s_out, h_out, held):
+    i = pl.program_id(0)
+
+    @pl.when(i == 0)
+    def _():
+        for n in range(0, TOKENS, TILE):
+            wide = x[n : n + TILE, :].astype(F32)
+            a_out[n : n + TILE, :] = (wide * scale_of(wide)).astype(BF16)
+
+    for n in range(0, TOKENS, TILE):
+        here = slice(n, n + TILE)
+        gate, up = dot(a_out[here, :], wg[...]), dot(a_out[here, :], wu[...])
         silu, slope = silu_and_slope(gate)
-        silu_out[:, at] = silu
-        slope_out[:, at] = up * slope
-        s_out[:, at] = (silu * up).astype(BF16)
-    h_out[...] = x[...] + dot(s_out[...], wd[...]).astype(BF16)
+        silu_out[here, :] = silu
+        slope_out[here, :] = up * slope
+        s = (silu * up).astype(BF16)
+        s_out[here, :] = s
+        held[here, pl.ds(pl.multiple_of(i * NARROW, NARROW), NARROW)] = s
+
+    @pl.when(i == SIXTHS - 1)
+    def _():
+        for n in range(0, TOKENS, TILE):
+            here = slice(n, n + TILE)
+            h_out[here, :] = x[here, :] + dot(held[here, :], wd[...]).astype(BF16)
 
 
 def turn_kernel(h, dy, wg, wu, wd, a_out, s_out, dg_out, du_out):
-    wide = h[...].astype(F32)
-    a = (wide * scale_of(wide)).astype(BF16)
-    a_out[...] = a
-    for c in range(PIECES):
-        at = slice(c * WIDE, (c + 1) * WIDE)
-        gate, up = dot(a, wg[:, at]), dot(a, wu[:, at])
-        d_s = dot(dy[...], wd[at, :], NT).astype(BF16).astype(F32)
+    @pl.when(pl.program_id(0) == 0)
+    def _():
+        for n in range(0, TOKENS, TILE):
+            wide = h[n : n + TILE, :].astype(F32)
+            a_out[n : n + TILE, :] = (wide * scale_of(wide)).astype(BF16)
+
+    for n in range(0, TOKENS, TILE):
+        here = slice(n, n + TILE)
+        gate, up = dot(a_out[here, :], wg[...]), dot(a_out[here, :], wu[...])
+        d_s = dot(dy[here, :], wd[...], NT).astype(BF16).astype(F32)
         silu, slope = silu_and_slope(gate)
-        s_out[:, at] = (silu * up).astype(BF16)
-        dg_out[:, at] = (d_s * (up * slope) * 2).astype(BF16)
-        du_out[:, at] = (d_s * silu).astype(BF16)
-
-
-def by_tiles(kernel, ins, weights, layer, outs, flops):
-    def tile(width):
-        return pl.BlockSpec((TILE, width), lambda i: (i, 0))
-
-    def whole(w):
-        return pl.BlockSpec((None, *w.shape[1:]), lambda i: (layer, 0, 0), pipeline_mode=pl.Buffered(1))
-
+        s_out[here, :] = (silu * up).astype(BF16)
+        dg_out[here, :] = (d_s * (up * slope) * 2).astype(BF16)
+        du_out[here, :] = (d_s * silu).astype(BF16)
+
+
+def by_columns(kernel, ins, weights, layer, outs, whole_down, scratch):
+    whole = pl.BlockSpec((TOKENS, D), lambda i: (0, 0), pipeline_mode=pl.Buffered(1))
+    across = pl.BlockSpec((None, D, NARROW), lambda i: (layer, 0, i))
+    if whole_down:
+        down = pl.BlockSpec((None, FF, D), lambda i: (layer, 0, 0), pipeline_mode=pl.Buffered(1))
+    else:
+        down = pl.BlockSpec((None, NARROW, D), lambda i: (layer, i, 0))
+    columns = pl.BlockSpec((TOKENS, NARROW), lambda i: (0, i))
     return pl.pallas_call(
         kernel,
-        grid=(TOKENS // TILE,),
-        in_specs=[tile(t.shape[1]) for t in ins] + [whole(w) for w in weights],
-        out_specs=[tile(width) for width, _ in outs],
+        grid=(SIXTHS,),
+        in_specs=[whole] * len(ins) + [across, across, down],
+        out_specs=[whole if width == D else columns for width, _ in outs],
         out_shape=[jax.ShapeDtypeStruct((TOKENS, width), dtype) for width, dtype in outs],
-        compiler_params=pltpu.CompilerParams(vmem_limit_bytes=62 * MIB),
-        cost_estimate=pl.CostEstimate(flops=flops, bytes_accessed=50 * MIB, transcendentals=0),
+        scratch_shapes=scratch,
+        compiler_params=pltpu.CompilerParams(vmem_limit_bytes=63 * MIB),
+        cost_estimate=pl.CostEstimate(flops=6 * TOKENS * D * FF, bytes_accessed=60 * MIB, transcendentals=0),
     )(*ins, *weights)
 
 
@@ -288,13 +304,6 @@
 
     load_a(a1).start()
     operand(0, start)
-    tile(0, start)
-    load_w(0).start()
-    load_w(1).start()
-    load_s(s1).start()
-    load_w(2).start()
-    for n in range(AHEAD):
-        hidden(n, start)
 
     def step(i, carry):
         slot = i % 2
@@ -303,13 +312,22 @@
         def _():
             operand(i, wait)
 
-            @pl.when((i + 1 < CHUNKS) & (i != 11))
-            def _():
-                operand(i + 1, start)
-
             @pl.when(i == 0)
             def _():
                 load_a(a1).wait()
+                tile(0, start)
+                load_w(0).start()
+                load_w(1).start()
+
+            @pl.when(i == 1)
+            def _():
+                load_s(s1).start()
+
+            @pl.when(i == 2)
+            def _():
+                load_w(2).start()
+                for n in range(AHEAD):
+                    hidden(n, start)
 
             @pl.when(i == 3)
             def _():
@@ -327,6 +345,10 @@
             @pl.when(i == 12)
             def _():
                 load_a(a0).wait()
+
+            @pl.when((i + 1 < CHUNKS) & (i != 11))
+            def _():
+                operand(i + 1, start)
 
             _, kind, _ = which(i)
 
@@ -560,13 +582,11 @@
 def solution(mesh):
     def step(x, dy, wg, wu, wd, *moments):
         x, dy = x[0], dy[0]
-        one = 2 * TOKENS * D * FF
-        a0, silu0, slope0, s0, h1 = by_tiles(
-            forward_kernel, (x,), (wg, wu, wd), 0, ((D, BF16), (FF, F32), (FF, F32), (FF, BF16), (D, BF16)), 3 * one
-        )
-        a1, s1, dg1, du1 = by_tiles(
-            turn_kernel, (h1, dy), (wg, wu, wd), 1, ((D, BF16), (FF, BF16), (FF, BF16), (FF, BF16)), 3 * one
-        )
+        weights = wg, wu, wd
+        kept = (D, BF16), (FF, F32), (FF, F32), (FF, BF16), (D, BF16)
+        a0, silu0, slope0, s0, h1 = by_columns(forward_kernel, (x,), weights, 0, kept, True, [pltpu.VMEM((TOKENS, FF), BF16)])
+        made = (D, BF16), (FF, BF16), (FF, BF16), (FF, BF16)
+        a1, s1, dg1, du1 = by_columns(turn_kernel, (h1, dy), weights, 1, made, False, [])
         return sum_and_step((a1, a0, s1, s0, dy, h1, dg1, du1, silu0, slope0), wg, wu, wd, *moments)
 
     whole, rows = P(None, None, None), P(None, "dp", None)

time: 350 us -> 347 us (level)
  no operation moved by 1% of the time
where the time goes in v4:
time: 347 us
  Pallas kernels  346 us (100%)
    pallas_call x1, Pallas kernels, sum_and_step(): pl.pallas_call(sum_kernel, in_specs=[any_] * 19, out_specs=[any_] * 11, o...  238 us
    pallas_call x2, Pallas kernels, by_columns(): pl.pallas_call(kernel, grid=(SIXTHS,), in_specs=[whole] * len(ins) + [acr...  84.7 us
    pallas_call x1, Pallas kernels, copied(): pl.pallas_call(copy_kernel, grid=(2 * COPIES,), in_specs=specs, out_specs...  23 us

profile of v4, /device:TPU:0, one launch (start us, length us, event | category | flops | bytes accessed | tf_op | source)
XLA Modules:
  0.0 346.8 jit_solution(12980621916858540510)
XLA Ops:
  0.6 43.6 %shard_map.178 = (bf16[2048,768]{1,0:T(8,128)(2,1)}, f32[2048,3072]{1,0:T(8,128)}, f32[2048,3072]{1,0:T(8,128)}, bf16[2048,3072]{1,0:T(8,128)(2,1)}, bf16[2048,768]{1,0:T(8,128)(2,1)}) custom-call(bf16[2048,768]{1,0:T(8,128)(2,1)} %bitcast.14, bf16[2,768,3072]{2,1,0:T(8,128)(2,1)} %refs_10_.1, bf16[2,768,3072]{2,1,0:T(8,128)(2,1)} %refs_11_.1, ...), custom_call_target="tpu_custom_call" | custom-call | flops 28991029248 | bytes 62914560 | tf_op jit(solution)/shard_map/pallas_call | solution.py:95
  44.3 41.1 %shard_map.179 = (bf16[2048,768]{1,0:T(8,128)(2,1)}, bf16[2048,3072]{1,0:T(8,128)(2,1)}, bf16[2048,3072]{1,0:T(8,128)(2,1)}, bf16[2048,3072]{1,0:T(8,128)(2,1)}) custom-call(bf16[2048,768]{1,0:T(8,128)(2,1)} %get-tuple-element.27.h.refs_5_, bf16[2048,768]{1,0:T(8,128)(2,1)} %bitcast.15, bf16[2,768,3072]{2,1,0:T(8,128)(2,1)} %refs_10_.1, ...), custom_call_target="tpu_custom_call" | custom-call | flops 28991029248 | bytes 62914560 | tf_op jit(solution)/shard_map/pallas_call | solution.py:95
  85.3 238.3 %shard_map.180 = (bf16[2,2,2,2,2,48,3072]{6,5,4,3,2,1,0:T(8,128)(2,1)}, bf16[2,2,2,2,2,48,3072]{6,5,4,3,2,1,0:T(8,128)(2,1)}, bf16[2,2,2,2,2,4,48,768]{7,6,5,4,3...) custom-call(bf16[2048,768]{1,0:T(8,128)(2,1)} %get-tuple-element.28., ...), custom_call_target="tpu_custom_call" | custom-call | flops 86973087744 | bytes 125829120 | tf_op jit(solution)/shard_map/pallas_call | solution.py:509
  323.6 23.0 %shard_map.181 = (bf16[2,768,3072]{2,1,0:T(8,128)(2,1)}, bf16[2,768,3072]{2,1,0:T(8,128)(2,1)}, bf16[2,3072,768]{2,1,0:T(8,128)(2,1)}, f32[2,48,3072]{2,1,0:T(8,...) custom-call(bf16[2,768,3072]{2,1,0:T(8,128)(2,1)} %bitcast.9, ...), custom_call_target="tpu_custom_call" | custom-call | tf_op jit(solution)/shard_map/pallas_call | solution.py:571
